TPU v7x, 256 devices: a whole 4x4x8 slice. The times are simulated.
256 devices in a mesh: grp: 8 (over x_hi, y), row: 32 (over z, x_lo, core).
Axes of the slice: x: 4 (x_hi: 2, x_lo: 2; x = x_hi * 2 + x_lo), y: 4, z: 8, core: 2. Of those that a mesh axis runs over, the one named last changes fastest.
Arguments:
- tables: bfloat16 [8, 32768, 512], P(None, 'row', 'grp'), may hold values from -1.1953125 to 1.1953125
- indices: int32 [4096, 8, 32], P('row', 'grp'), may hold values from 0 to 32767
- block_shift: int32 [8], replicated, may hold values from 0 to 31
- pooled_grad: bfloat16 [4096, 8, 512], P('row', 'grp'), may hold values from -6 to 6
Outputs:
- pooled: bfloat16 [4096, 8, 512], P('row', 'grp')
- updated: bfloat16 [8, 32768, 512], P('grp', 'row')
All inputs are finite; a program needn't handle non-finite values.
Results may differ from a plain program's by a relative error of at most 0.001.
Values may be sent and summed in bfloat16 or wider, within the bound.
No kernel may reach another device: no remote copies, remote signals or barrier semaphores. Data moves between devices by JAX's collectives and lax.ppermute only.
A program may use at most 64 MiB of HBM per device.

v0:
```python
import math

import jax
import jax.numpy as jnp
from jax import lax
from jax.sharding import PartitionSpec as P

step_rate = 0.25


def roll_rows(values, amount):
    return jnp.roll(values, amount, axis=0)


def table_pass(table_rows, lookups, upstream, block_start):
    total = lookups.shape[0]
    bag_size = lookups.shape[1]
    block_rows, lane_count = table_rows.shape
    sample_block = math.gcd(512, total)
    block_count = total // sample_block
    positions = lax.iota(jnp.int32, block_rows)

    def accumulate(running, pieces_in):
        lookup_block, upstream_block = pieces_in
        offsets = lookup_block - block_start
        counts = jnp.zeros((sample_block, block_rows), jnp.int32)
        for group_start in range(0, bag_size, 4):
            hits = offsets[:, group_start : group_start + 4, None] == positions[None, None, :]
            counts = counts + jnp.sum(hits, axis=1, dtype=jnp.int32)
        weights = counts.astype(jnp.bfloat16)
        partial_pool = jnp.dot(weights, table_rows, preferred_element_type=jnp.float32)
        running = running + lax.dot_general(
            weights, upstream_block, (((0,), (0,)), ((), ())), preferred_element_type=jnp.float32
        )
        return (running, partial_pool)

    start_grad = jnp.zeros((block_rows, lane_count), jnp.float32)
    running, partials = lax.scan(
        accumulate,
        start_grad,
        (
            lookups.reshape(block_count, sample_block, bag_size),
            upstream.reshape(block_count, sample_block, lane_count),
        ),
    )
    return (running, partials.reshape(total, lane_count))


def per_device(tables, indices, block_shift, pooled_grad):
    regrouped = lax.all_to_all(tables, "grp", split_axis=0, concat_axis=2, tiled=True)
    table_count, block_rows, lane_count = regrouped.shape
    row_count = lax.axis_size("row")
    row_index = lax.axis_index("row")
    first_table = lax.axis_index("grp") * table_count
    table_shifts = lax.dynamic_slice_in_dim(block_shift, first_table, table_count)
    piece_rows = block_rows // row_count
    pieces = regrouped.reshape(table_count, row_count, piece_rows, lane_count)
    scattered = lax.all_to_all(pieces, "row", split_axis=1, concat_axis=1, tiled=True)
    reordered = jax.vmap(roll_rows)(scattered, table_shifts)
    rotated = lax.all_to_all(reordered, "row", split_axis=1, concat_axis=1, tiled=True).reshape(
        table_count, block_rows, lane_count
    )
    gathered_ids, gathered_grad = (
        lax.all_gather(indices, "row", axis=0, tiled=True),
        lax.all_gather(pooled_grad, "row", axis=0, tiled=True),
    )
    owned_starts = (row_index - table_shifts) % row_count * block_rows
    running, partials = table_pass(
        rotated[0], gathered_ids[:, 0, :], gathered_grad[:, 0, :], owned_starts[0]
    )
    gradients = [running]
    partial_list = [partials]
    stacked = jnp.stack(partial_list, axis=1)
    pooled = lax.psum_scatter(stacked, "row", scatter_dimension=0, tiled=True).astype(jnp.bfloat16)
    gradient = jnp.stack(gradients, axis=0)
    updated = (rotated.astype(jnp.float32) - step_rate * gradient).astype(jnp.bfloat16)
    return (pooled, updated)


def solution(mesh):
    placed = (P(None, "row", "grp"), P("row", "grp", None), P(), P("row", "grp", None))
    return jax.shard_map(
        per_device,
        mesh=mesh,
        in_specs=placed,
        out_specs=(P("row", "grp", None), P("grp", "row", None)),
        check_vma=False,
    )
```

profile of v0, /device:TPU:4, one launch (start us, length us, event | category | flops | bytes accessed | tf_op | source)
XLA Modules:
  0.0 465.5 jit_solution(8250286337026694767)
XLA Ops:
  7.9 23.1 %all_to_all.25 = bf16[8,1024,64]{1,2,0:T(8,128)(2,1)S(1)} all-to-all(bf16[8,1024,64]{1,2,0:T(8,128)(2,1)} %param.6), channel_id=1, replica_groups=mesh['grp'=8,'row'=32] {'grp'}, dimensions={0} | all-to-all | bytes 2097152 | tf_op jit(solution)/shard_map/all_to_all | solution.py:50
  34.7 9.6 %all-to-all-start.1 = ((bf16[1,32,32,512]{3,2,0,1:T(8,128)(2,1)}), bf16[1,32,32,512]{3,2,0,1:T(8,128)(2,1)S(1)}, u32[]{:S(2)}, u32[]{:S(2)}) async-start(bf16[1,32,32,512]{3,2,0,1:T(8,128)(2,1)} %bitcast.5), calls=%async_computation.1 | async-start | bytes 2097152 | tf_op jit(solution)/shard_map/all_to_all | solution.py:58
  46.8 34.6 %all-to-all-done.1 = bf16[1,32,32,512]{3,2,0,1:T(8,128)(2,1)S(1)} async-done(((bf16[1,32,32,512]{3,2,0,1:T(8,128)(2,1)}), bf16[1,32,32,512]{3,2,0,1:T(8,128)(2,1)S(1)}, u32[]{:S(2)}, u32[]{:S(2)}) %all-to-all-start.1) | async-done | bytes 1048608 | tf_op jit(solution)/shard_map/all_to_all | solution.py:58
  82.7 5.2 %all-to-all-start.2 = ((bf16[1,32,32,512]{3,2,0,1:T(8,128)(2,1)}), bf16[1,32,32,512]{3,2,0,1:T(8,128)(2,1)}, u32[]{:S(2)}, u32[]{:S(2)}) async-start(bf16[1,32,32,512]{3,2,0,1:T(8,128)(2,1)} %fusion.8), calls=%async_computation.2 | async-start | bytes 2097152 | tf_op jit(solution)/shard_map/all_to_all | solution.py:60
  88.6 51.6 %all_gather.6 = s32[4096,1,32]{0,2,1:T(8,128)S(1)} all-gather(s32[128,1,32]{0,2,1:T(8,128)S(1)} %copy-done.3), channel_id=1, replica_groups=mesh['grp'=8,'row'=32] {'row'}, dimensions={0}, use_global_device_ids=true | all-gather | bytes 540672 | tf_op jit(solution)/shard_map/all_gather | solution.py:64
  141.3 182.9 %while.15 = (s32[]{:T(128)}, f32[1024,512]{1,0:T(8,128)}, f32[8,512,512]{2,1,0:T(8,128)}, s32[8,512,32]{1,0,2:T(8,128)}, s32[]{:T(128)}, /*index=5*/bf16[8,512,5...) while((s32[]{:T(128)}, f32[1024,512]{1,0:T(8,128)}, ...), condition=%wide.region_9.10_spmd.clone.clone, body=%wide.region_0.9_spmd.clone.clone.sunk | while | flops 1125138432 | bytes 60753060 | solution.py:38
  142.4 3.3 convert_reduce_fusion.13
  145.7 3.3 convert_reduce_fusion.14
  149.0 3.3 convert_reduce_fusion.15
  152.3 3.3 convert_reduce_fusion.12
  165.3 3.3 convert_reduce_fusion.13
  168.6 3.3 convert_reduce_fusion.14
  171.9 3.3 convert_reduce_fusion.15
  175.2 3.3 convert_reduce_fusion.12
  188.2 3.3 convert_reduce_fusion.13
  191.5 3.3 convert_reduce_fusion.14
  194.8 3.3 convert_reduce_fusion.15
  198.1 3.3 convert_reduce_fusion.12
  211.0 3.3 convert_reduce_fusion.13
  214.3 3.3 convert_reduce_fusion.14
  217.6 3.3 convert_reduce_fusion.15
  220.9 3.3 convert_reduce_fusion.12
  233.9 3.3 convert_reduce_fusion.13
  328.3 128.8 %reduce-scatter.2.cloned.1.call-done = f32[128,1,512]{2,0,1:T(8,128)} async-done(((f32[4096,1,512]{2,0,1:T(8,128)}), f32[128,1,512]{2,0,1:T(8,128)}) %reduce-scatter.2.cloned.1.call-update) | async-done | bytes 262160 | tf_op jit(solution)/shard_map/reduce_scatter | solution.py:74
  (116 shorter events, 139.6 us)
Async XLA Ops:
  7.2 134.1 %all-gather.2.cloned.1.call-start = ((), (), s32[]{:S(2)}) async-start(), calls=%async_computation.4 | async-start | bytes 4325376 | tf_op jit(solution)/shard_map/all_gather | solution.py:65
  32.6 11.7 %copy-start.4 = (s32[8]{0:T(128)S(1)}, s32[8]{0:T(128)}, u32[]{:S(2)}) copy-start(s32[8]{0:T(128)} %param.8) | copy-start | bytes 100
  34.7 46.7 %all-to-all-start.1 = ((bf16[1,32,32,512]{3,2,0,1:T(8,128)(2,1)}), bf16[1,32,32,512]{3,2,0,1:T(8,128)(2,1)S(1)}, u32[]{:S(2)}, u32[]{:S(2)}) async-start(bf16[1,32,32,512]{3,2,0,1:T(8,128)(2,1)} %bitcast.5), calls=%async_computation.1 | async-start | bytes 2097152 | tf_op jit(solution)/shard_map/all_to_all | solution.py:58
  81.4 7.3 %copy-start.3 = (s32[128,1,32]{0,2,1:T(8,128)S(1)}, s32[128,1,32]{0,2,1:T(8,128)}, u32[]{:S(2)}) copy-start(s32[128,1,32]{0,2,1:T(8,128)} %param.7) | copy-start | bytes 49156
  82.7 58.6 %all-to-all-start.2 = ((bf16[1,32,32,512]{3,2,0,1:T(8,128)(2,1)}), bf16[1,32,32,512]{3,2,0,1:T(8,128)(2,1)}, u32[]{:S(2)}, u32[]{:S(2)}) async-start(bf16[1,32,32,512]{3,2,0,1:T(8,128)(2,1)} %fusion.8), calls=%async_computation.2 | async-start | bytes 2097152 | tf_op jit(solution)/shard_map/all_to_all | solution.py:60
  87.9 369.1 %reduce-scatter.2.cloned.1.call-start = ((), (), s32[]{:S(2)}) async-start(), calls=%async_computation.5 | async-start | bytes 8650752 | tf_op jit(solution)/shard_map/reduce_scatter | solution.py:74
  157.7 3.1 copy-start
  162.8 1.4 copy-start.1
  180.6 3.1 copy-start
  185.7 1.4 copy-start.1
  203.5 3.1 copy-start
  208.5 1.4 copy-start.1
  226.3 3.1 copy-start
  231.4 1.4 copy-start.1
  249.2 3.1 copy-start
  254.2 1.4 copy-start.1
  272.0 3.1 copy-start
  277.1 1.4 copy-start.1
  294.9 3.1 copy-start
  300.0 1.4 copy-start.1
  317.8 3.1 copy-start
  322.8 1.4 copy-start.1
  324.2 1.6 copy-start.2
Sparse Core Ops, SparseCore 0:
  9.8 80.0 all-gather.1
  324.3 132.6 reduce-scatter.1
where the time goes:
time: 467 us; the launch traced here: 466 us
  waiting for transfers between devices  164 us (35%)
  other arithmetic  128 us (27%)
  blocking collectives  74.6 us (16%)
  matrix products  40.3 us (9%)
  local copies, waits for them, and re-layouts  26.7 us (6%)
  between operations  16.6 us (4%)
  starting transfers between devices  14.9 us (3%)
    reduce_scatter x1, waiting for transfers between devices, per_device(): lax.psum_scatter(stacked, 'row', scatter_dimension=0, tiled=True)  129 us
    reduce_sum x32, other arithmetic, accumulate(): counts = counts + jnp.sum(hits, axis=1, dtype=jnp.int32)  105 us
    all_gather x1, blocking collectives, per_device(): lax.all_gather(indices, 'row', axis=0, tiled=True)  51.6 us
    all_to_all x1, waiting for transfers between devices, per_device(): lax.all_to_all(pieces, 'row', split_axis=1, concat_axis=1, tiled=True)  34.6 us
    dot_general x8, matrix products, accumulate(): jnp.dot(weights, table_rows, preferred_element_type=jnp.float32)  24.7 us
    all_to_all x1, blocking collectives, per_device(): lax.all_to_all(tables, 'grp', split_axis=0, concat_axis=2, tiled=True)  23.1 us
    convert_element_type x8, other arithmetic, accumulate(): weights = counts.astype(jnp.bfloat16)  16.8 us
    dot_general x8, matrix products, accumulate(): lax.dot_general(weights, upstream_block, (((0,), (0,)), ((), ())), prefer...  15.6 us
  transfers between devices with their start and end apart: 4, of which 2 were waited for; matrix products, arithmetic and copies ran while one was open for 2% of the time, Pallas kernels for 0%

commit v1 on v0

v1 whole, which is shorter than its diff:
```python
import jax
import jax.numpy as jnp
from jax import lax
from jax.experimental import pallas as pl
from jax.experimental.pallas import tpu as pltpu
from jax.sharding import Mesh, PartitionSpec as P

STEP_RATE = 0.25
ROW = ("z", "xl", "core")
BLOCK = 1024
PIECE = 32
WINDOW = 256
STATIC_HITS = 4


def count_kernel(keys_ref, out_ref, hits_ref):
    window = pl.program_id(1)
    bag = keys_ref.shape[0]
    empty = jnp.full(keys_ref.shape[1:], -1, jnp.int32)
    hits = []
    total = jnp.zeros(keys_ref.shape[1:], jnp.int32)
    for k in range(bag):
        key = keys_ref[k]
        mine = (key >> 8) == window
        hits.append(empty)
        for j in range(k, 0, -1):
            hits[j] = jnp.where(mine, hits[j - 1], hits[j])
        hits[0] = jnp.where(mine, key & 255, hits[0])
        total = total + jnp.where(mine, 1, 0)
    for j in range(bag):
        hits_ref[j] = hits[j].astype(jnp.float32)
    most = jnp.max(total)
    rows = lax.broadcasted_iota(jnp.int32, (WINDOW, 128), 0).astype(jnp.bfloat16)
    one = jnp.ones((WINDOW, 128), jnp.bfloat16)
    zero = jnp.zeros((WINDOW, 128), jnp.bfloat16)

    def marks(j, d):
        wanted = jnp.broadcast_to(hits_ref[j, pl.ds(d, 1), :], (WINDOW, 128)).astype(jnp.bfloat16)
        return jnp.where(rows == wanted, one, zero)

    for d in range(keys_ref.shape[1]):
        counts = marks(0, d)
        for j in range(1, STATIC_HITS):
            counts = counts + marks(j, d)
        out_ref[:, d * 128 : (d + 1) * 128] = counts

    def more(j, carry):
        for d in range(keys_ref.shape[1]):
            out_ref[:, d * 128 : (d + 1) * 128] += marks(j, d)
        return carry

    lax.fori_loop(STATIC_HITS, most, more, 0)


def count_lookups(keys, rows):
    bag, owners, lanes = keys.shape
    groups = owners // 8
    return pl.pallas_call(
        count_kernel,
        grid=(groups, rows // WINDOW),
        in_specs=[pl.BlockSpec((bag, 8, lanes), lambda g, w: (0, g, 0))],
        out_specs=pl.BlockSpec((WINDOW, 8 * lanes), lambda g, w: (w, g)),
        out_shape=jax.ShapeDtypeStruct((rows, owners * lanes), jnp.bfloat16),
        scratch_shapes=[pltpu.VMEM((bag, 8, lanes), jnp.float32)],
        name="count_lookups",
    )(keys)


def pool_kernel(t0, t1, t2, t3, w_ref, out_ref):
    total = jnp.dot(t0[...], w_ref[0:BLOCK, :], preferred_element_type=jnp.float32)
    for q, t in enumerate((t1, t2, t3), 1):
        total += jnp.dot(t[...], w_ref[q * BLOCK : (q + 1) * BLOCK, :], preferred_element_type=jnp.float32)
    for half in range(2):
        out_ref[half] = total[:, half * 128 : (half + 1) * 128]


def pool(tables, counts):
    dim = tables[0].shape[0]
    samples = counts.shape[1]
    whole = pl.BlockSpec((dim, BLOCK), lambda n: (0, 0))
    return pl.pallas_call(
        pool_kernel,
        grid=(samples // 256,),
        in_specs=[whole] * 4 + [pl.BlockSpec((4 * BLOCK, 256), lambda n: (0, n))],
        out_specs=pl.BlockSpec((2, dim, 128), lambda n: (n, 0, 0)),
        out_shape=jax.ShapeDtypeStruct((samples // 128, dim, 128), jnp.float32),
        name="pool",
    )(*tables, counts)


def per_device(tables, indices, block_shift, pooled_grad):
    z, xl, core = (lax.axis_index(a) for a in ROW)
    me = 4 * z + 2 * xl + core
    shift = lax.dynamic_index_in_dim(block_shift, lax.axis_index("grp"), keepdims=False)
    swap = [(0, 1), (1, 0)]

    grads = lax.all_gather(pooled_grad[:, 0, :], ROW, axis=0, tiled=True)

    columns = lax.all_to_all(jnp.swapaxes(tables, 1, 2), "grp", 0, 0, tiled=True).reshape(-1, BLOCK)

    ids = indices[:, 0, :].T.astype(jnp.int16)
    ids = lax.all_to_all(jnp.broadcast_to(ids, (32,) + ids.shape), ROW, 0, 0, tiled=True)
    ids = jnp.swapaxes(ids.astype(jnp.int32), 0, 1)

    mine = lax.dynamic_index_in_dim(ids.reshape(32, 8, 4, 128), 2 * xl + core, axis=2, keepdims=False)
    near = ((mine >> 10) & 3) ^ (2 * xl + core)
    pool_keys = jnp.where((mine >> 12) == z, (near << 10) | (mine & 1023), -1)
    pool_counts = count_lookups(pool_keys, 4 * BLOCK)
    across_core = lax.ppermute(columns, "core", swap)
    across_xl = lax.ppermute(columns, "xl", swap)
    across_both = lax.ppermute(across_xl, "core", swap)
    partial = pool((columns, across_core, across_xl, across_both), pool_counts)
    pooled = lax.psum_scatter(partial, "z", scatter_dimension=0, tiled=True)[0]
    pooled = pooled.T.astype(jnp.bfloat16)[:, None, :]

    pieces = lax.all_to_all(columns.T.reshape(32, PIECE, -1), ROW, 0, 0, tiled=True)
    pieces = jnp.roll(pieces, shift, axis=0).reshape(BLOCK, -1)
    place = ((ids >> 10) + shift) & 31
    update_keys = jnp.where(((ids >> 5) & 31) == me, (place << 5) | (ids & 31), -1)
    update_counts = count_lookups(update_keys, BLOCK)
    gradient = jnp.dot(update_counts, grads, preferred_element_type=jnp.float32)
    fresh = (pieces.astype(jnp.float32) - STEP_RATE * gradient).astype(jnp.bfloat16)
    updated = lax.all_to_all(fresh.reshape(32, PIECE, -1), ROW, 0, 0, tiled=True)
    return pooled, updated.reshape(1, BLOCK, -1)


def solution(mesh):
    split = Mesh(mesh.devices.reshape(8, 8, 2, 2), ("grp",) + ROW)
    return jax.shard_map(
        per_device,
        mesh=split,
        in_specs=(P(None, ROW, "grp"), P(ROW, "grp", None), P(), P(ROW, "grp", None)),
        out_specs=(P(ROW, "grp", None), P("grp", ROW, None)),
        check_vma=False,
    )
```

time: 467 us -> 189 us (0.40)
  other arithmetic: 128 us -> 4.61 us
  waiting for transfers between devices: 164 us -> 86.6 us
  blocking collectives: 74.6 us -> 0 us
  Pallas kernels: 0 us -> 34.2 us
  matrix products: 40.3 us -> 10.1 us
  local copies, waits for them, and re-layouts: 26.7 us -> 4.63 us
  starting transfers between devices: 14.9 us -> 27.9 us
    reduce_scatter x1, waiting for transfers between devices: 129 us -> 13.9 us  [per_device(): pooled = lax.psum_scatter(partial, 'z', scatter_dimension=0, tiled=True)[0]]
    reduce_sum x32 -> x0, other arithmetic: 105 us -> none  [accumulate(): counts = counts + jnp.sum(hits, axis=1, dtype=jnp.int32)]
    all_gather x1 -> x0, blocking collectives: 51.6 us -> none  [per_device(): lax.all_gather(indices, 'row', axis=0, tiled=True)]
    pallas_call x0 -> x3, Pallas kernels: none -> 34.2 us  [the longest x2 24.8 us: count_lookups(): pl.pallas_call(count_kernel, grid=(groups, rows // WINDOW), in_specs=[pl....]
    ppermute x0 -> x3, waiting for transfers between devices: none -> 33.2 us  [the longest x1 33.2 us: per_device(): across_xl = lax.ppermute(columns, 'xl', swap)]
    dot_general x16 -> x1, matrix products: 40.3 us -> 10.1 us  [per_device(): gradient = jnp.dot(update_counts, grads, preferred_element_type=jnp.float32)]
    all_to_all x1 -> x0, blocking collectives: 23.1 us -> none  [per_device(): lax.all_to_all(tables, 'grp', split_axis=0, concat_axis=2, tiled=True)]
    convert_element_type x10 -> x1, other arithmetic: 21 us -> 0.72 us  [per_device(): ids = indices[:, 0, :].T.astype(jnp.int16)]
  transfers between devices with their start and end apart: 4 -> 9, of which waited for: 2 -> 5; matrix products, arithmetic and copies ran while one was open for 2% -> 10% of each run, Pallas kernels for 0% -> 18%
where the time goes in v1:
time: 189 us; the launch traced here: 186 us
  waiting for transfers between devices  86.6 us (46%)
  Pallas kernels  34.2 us (18%)
  starting transfers between devices  27.9 us (15%)
  between operations  17.5 us (9%)
  matrix products  10.1 us (5%)
  local copies, waits for them, and re-layouts  4.63 us (2%)
  other arithmetic  4.61 us (2%)
    ppermute x1, waiting for transfers between devices, per_device(): across_xl = lax.ppermute(columns, 'xl', swap)  33.2 us
    pallas_call x2, Pallas kernels, count_lookups(): pl.pallas_call(count_kernel, grid=(groups, rows // WINDOW), in_specs=[pl....  24.8 us
    all_to_all x1, waiting for transfers between devices, per_device(): lax.all_to_all(fresh.reshape(32, PIECE, -1), ROW, 0, 0, tiled=True)  14.1 us
    reduce_scatter x1, waiting for transfers between devices, per_device(): pooled = lax.psum_scatter(partial, 'z', scatter_dimension=0, tiled=True)[0]  13.9 us
    all_to_all x1, waiting for transfers between devices, per_device(): lax.all_to_all(jnp.swapaxes(tables, 1, 2), 'grp', 0, 0, tiled=True)  13.5 us
    all_to_all x1, waiting for transfers between devices, per_device(): lax.all_to_all(jnp.broadcast_to(ids, (32,) + ids.shape), ROW, 0, 0, tiled...  11.2 us
    dot_general x1, matrix products, per_device(): gradient = jnp.dot(update_counts, grads, preferred_element_type=jnp.float32)  10.1 us
    all_to_all x1, starting transfers between devices, per_device(): lax.all_to_all(jnp.broadcast_to(ids, (32,) + ids.shape), ROW, 0, 0, tiled...  9.89 us
  transfers between devices with their start and end apart: 9, of which 5 were waited for; matrix products, arithmetic and copies ran while one was open for 10% of the time, Pallas kernels for 18%

profile of v1, /device:TPU:4, one launch (start us, length us, event | category | flops | bytes accessed | tf_op | source)
XLA Modules:
  0.0 185.6 jit_solution(17579547012019890486)
XLA Ops:
  8.0 0.7 all-gather.3.cloned.1.call-update
  8.7 7.4 %all-to-all-start = ((bf16[8,64,1024]{2,1,0:T(8,128)(2,1)}), bf16[8,64,1024]{2,1,0:T(8,128)(2,1)S(1)}, u32[]{:S(2)}, u32[]{:S(2)}) async-start(bf16[8,64,1024]{2,1,0:T(8,128)(2,1)} %bitcast.59), calls=%async_computation | async-start | bytes 2097152 | tf_op jit(solution)/shard_map/all_to_all | solution.py:99
  16.2 0.7 convert_bitcast_fusion.1
  16.9 13.5 %all-to-all-done = bf16[8,64,1024]{2,1,0:T(8,128)(2,1)S(1)} async-done(((bf16[8,64,1024]{2,1,0:T(8,128)(2,1)}), bf16[8,64,1024]{2,1,0:T(8,128)(2,1)S(1)}, u32[]{:S(2)}, u32[]{:S(2)}) %all-to-all-start) | async-done | bytes 1048608 | tf_op jit(solution)/shard_map/all_to_all | solution.py:99
  30.4 0.8 broadcast_in_dim.14
  31.2 9.9 %all-to-all-start.1 = ((s16[32,32,128]{2,1,0:T(8,128)(2,1)}), s16[32,32,128]{2,1,0:T(8,128)(2,1)S(1)}, u32[]{:S(2)}, u32[]{:S(2)}) async-start(s16[32,32,128]{2,1,0:T(8,128)(2,1)} %broadcast_in_dim.14), calls=%async_computation.1 | async-start | bytes 524288 | tf_op jit(solution)/shard_map/all_to_all | solution.py:102
  41.1 1.9 %collective-permute-start.1 = (bf16[512,1024]{1,0:T(8,128)(2,1)S(1)}, bf16[512,1024]{1,0:T(8,128)(2,1)S(1)}, u32[]{:S(2)}, u32[]{:S(2)}) collective-permute-start(bf16[512,1024]{1,0:T(8,128)(2,1)S(1)} %bitcast.53), channel_id=1, source_target_pairs={{0,2},{2,0},{1,3},{3,1},{4,6},{6,4},{5,7},{7,5},{8,10},{10,8},{9,1... | collective-permute-start | bytes 3145736 | tf_op jit(solution)/shard_map/ppermute | solution.py:110
  43.0 1.4 copy.14
  44.3 11.2 %all-to-all-done.1 = s16[32,32,128]{2,1,0:T(8,128)(2,1)S(1)} async-done(((s16[32,32,128]{2,1,0:T(8,128)(2,1)}), s16[32,32,128]{2,1,0:T(8,128)(2,1)S(1)}, u32[]{:S(2)}, u32[]{:S(2)}) %all-to-all-start.1) | async-done | bytes 262176 | tf_op jit(solution)/shard_map/all_to_all | solution.py:102
  55.6 3.9 %all-to-all-start.2 = ((bf16[32,32,512]{2,1,0:T(8,128)(2,1)}), bf16[32,32,512]{2,1,0:T(8,128)(2,1)S(1)}, u32[]{:S(2)}, u32[]{:S(2)}) async-start(bf16[32,32,512]{2,1,0:T(8,128)(2,1)} %bitcast.11), calls=%async_computation.3 | async-start | bytes 2097152 | tf_op jit(solution)/shard_map/all_to_all | solution.py:116
  59.8 33.2 %collective-permute-done.1.t2 = bf16[512,1024]{1,0:T(8,128)(2,1)S(1)} collective-permute-done((bf16[512,1024]{1,0:T(8,128)(2,1)S(1)}, bf16[512,1024]{1,0:T(8,128)(2,1)S(1)}, u32[]{:S(2)}, u32[]{:S(2)}) %collective-permute-start.1) | collective-permute-done | bytes 1048608 | tf_op jit(solution)/shard_map/ppermute | solution.py:110
  93.3 0.7 select_bitcast_fusion.keys_ref
  94.0 11.9 %count_lookups.2.w_ref = bf16[4096,1024]{1,0:T(8,128)(2,1)} custom-call(s32[32,8,128]{2,1,0:T(8,128)} %select_bitcast_fusion.keys_ref), custom_call_target="tpu_custom_call" | custom-call | tf_op jit(solution)/shard_map/count_lookups/pallas_call | solution.py:58
  106.0 9.3 %pool.1 = f32[8,512,128]{2,1,0:T(8,128)} custom-call(bf16[512,1024]{1,0:T(8,128)(2,1)} %bitcast.56, bf16[512,1024]{1,0:T(8,128)(2,1)} %collective-permute-done.t1, bf16[512,1024]{1,0:T(8,128)(2,1)} %copy-done.1, bf16[512,1024]{1,0:T(8,128)(2,1)} %collective-permute-done.2.t3, bf16[4096,1024]{1,0:T(8,128)(2,1)} %count_lookups.2.w_ref), custom_call_target="tpu_custom_call" | custom-call | tf_op jit(solution)/shard_map/pool/pallas_call | solution.py:81
  115.3 0.6 dynamic_slice.13
  117.9 1.7 fusion.7.keys_ref
  119.6 12.9 %count_lookups.3 = bf16[1024,4096]{1,0:T(8,128)(2,1)} custom-call(s32[32,32,128]{2,1,0:T(8,128)} %fusion.7.keys_ref), custom_call_target="tpu_custom_call" | custom-call | tf_op jit(solution)/shard_map/count_lookups/pallas_call | solution.py:58
  132.9 10.1 %fusion.2 = bf16[1024,512]{1,0:T(8,128)(2,1)} fusion(bf16[1024,512]{1,0:T(8,128)(2,1)S(1)} %bitcast.58, bf16[1024,4096]{1,0:T(8,128)(2,1)} %count_lookups.3, bf16[4096,1,512]{2,0,1:T(8,128)(2,1)} %all-gather.3.cloned.1.call-done), kind=kOutput, calls=%fused_computation.5 | convolution fusion | flops 4297064448 | bytes 14680064 | tf_op jit(solution)/shard_map/dot_general | solution.py:121
  143.0 4.4 %all-to-all-start.3 = ((bf16[32,32,512]{2,1,0:T(8,128)(2,1)}), bf16[32,32,512]{2,1,0:T(8,128)(2,1)S(1)}, u32[]{:S(2)}, u32[]{:S(2)}) async-start(bf16[32,32,512]{2,1,0:T(8,128)(2,1)} %bitcast.15), calls=%async_computation.4 | async-start | bytes 2097152 | tf_op jit(solution)/shard_map/all_to_all | solution.py:123
  147.5 13.9 %reduce-scatter.2.cloned.1.call-done = f32[1,512,128]{2,1,0:T(8,128)} async-done(((f32[8,512,128]{2,1,0:T(8,128)}), f32[1,512,128]{2,1,0:T(8,128)}) %reduce-scatter.2.cloned.1.call-update) | async-done | bytes 262160 | tf_op jit(solution)/shard_map/reduce_scatter | solution.py:113
  161.4 1.0 convert_bitcast_fusion
  162.3 0.8 copy.15
  163.1 14.1 %all-to-all-done.3 = bf16[32,32,512]{2,1,0:T(8,128)(2,1)S(1)} async-done(((bf16[32,32,512]{2,1,0:T(8,128)(2,1)}), bf16[32,32,512]{2,1,0:T(8,128)(2,1)S(1)}, u32[]{:S(2)}, u32[]{:S(2)}) %all-to-all-start.3) | async-done | bytes 1048608 | tf_op jit(solution)/shard_map/all_to_all | solution.py:123
  177.2 1.0 copy.21
  (18 shorter events, 1.0 us)
Async XLA Ops:
  8.0 124.9 %all-gather.3.cloned.1.call-start = ((), (), s32[]{:S(2)}) async-start(), calls=%async_computation.6 | async-start | bytes 4325376 | tf_op jit(solution)/shard_map/all_gather | solution.py:97
  8.7 21.7 %all-to-all-start = ((bf16[8,64,1024]{2,1,0:T(8,128)(2,1)}), bf16[8,64,1024]{2,1,0:T(8,128)(2,1)S(1)}, u32[]{:S(2)}, u32[]{:S(2)}) async-start(bf16[8,64,1024]{2,1,0:T(8,128)(2,1)} %bitcast.59), calls=%async_computation | async-start | bytes 2097152 | tf_op jit(solution)/shard_map/all_to_all | solution.py:99
  30.4 75.5 %copy-start = (bf16[8,64,1024]{2,1,0:T(8,128)(2,1)}, bf16[8,64,1024]{2,1,0:T(8,128)(2,1)S(1)}, u32[]{:S(2)}) copy-start(bf16[8,64,1024]{2,1,0:T(8,128)(2,1)S(1)} %all-to-all-done) | copy-start | bytes 3145732
  31.2 24.4 %all-to-all-start.1 = ((s16[32,32,128]{2,1,0:T(8,128)(2,1)}), s16[32,32,128]{2,1,0:T(8,128)(2,1)S(1)}, u32[]{:S(2)}, u32[]{:S(2)}) async-start(s16[32,32,128]{2,1,0:T(8,128)(2,1)} %broadcast_in_dim.14), calls=%async_computation.1 | async-start | bytes 524288 | tf_op jit(solution)/shard_map/all_to_all | solution.py:102
  41.1 51.9 %collective-permute-start.1 = (bf16[512,1024]{1,0:T(8,128)(2,1)S(1)}, bf16[512,1024]{1,0:T(8,128)(2,1)S(1)}, u32[]{:S(2)}, u32[]{:S(2)}) collective-permute-start(bf16[512,1024]{1,0:T(8,128)(2,1)S(1)} %bitcast.53), channel_id=1, source_target_pairs={{0,2},{2,0},{1,3},{3,1},{4,6},{6,4},{5,7},{7,5},{8,10},{10,8},{9,1... | collective-permute-start | bytes 3145736 | tf_op jit(solution)/shard_map/ppermute | solution.py:110
  55.6 76.9 %all-to-all-start.2 = ((bf16[32,32,512]{2,1,0:T(8,128)(2,1)}), bf16[32,32,512]{2,1,0:T(8,128)(2,1)S(1)}, u32[]{:S(2)}, u32[]{:S(2)}) async-start(bf16[32,32,512]{2,1,0:T(8,128)(2,1)} %bitcast.11), calls=%async_computation.3 | async-start | bytes 2097152 | tf_op jit(solution)/shard_map/all_to_all | solution.py:116
  59.5 101.9 %reduce-scatter.2.cloned.1.call-start = ((), (), s32[]{:S(2)}) async-start(), calls=%async_computation.5 | async-start | bytes 2359296 | tf_op jit(solution)/shard_map/reduce_scatter | solution.py:113
  59.6 46.4 %collective-permute-start = (bf16[512,1024]{1,0:T(8,128)(2,1)S(1)}, bf16[512,1024]{1,0:T(8,128)(2,1)}, u32[]{:S(2)}, u32[]{:S(2)}) collective-permute-start(bf16[512,1024]{1,0:T(8,128)(2,1)S(1)} %bitcast.55), channel_id=1, source_target_pairs={{0,1},{1,0},{2,3},{3,2},{4,5},{5,4},{6,7},{7,6},{8,9},{9,8},{10,11... | collective-permute-start | bytes 3145736 | tf_op jit(solution)/shard_map/ppermute | solution.py:109
  93.0 12.9 %copy-start.1 = (bf16[512,1024]{1,0:T(8,128)(2,1)}, bf16[512,1024]{1,0:T(8,128)(2,1)S(1)}, u32[]{:S(2)}) copy-start(bf16[512,1024]{1,0:T(8,128)(2,1)S(1)} %collective-permute-done.1.t2) | copy-start | bytes 3145732
  93.0 13.0 %collective-permute-start.2 = (bf16[512,1024]{1,0:T(8,128)(2,1)S(1)}, bf16[512,1024]{1,0:T(8,128)(2,1)}, u32[]{:S(2)}, u32[]{:S(2)}) collective-permute-start(bf16[512,1024]{1,0:T(8,128)(2,1)S(1)} %collective-permute-done.1.t2), channel_id=1, source_target_pairs={{0,1},{1,0},{2,3},{3,2},{4,5},{5,4},{6,7},{7,6},{8,9},{9,8},{10,11... | collective-permute-start | bytes 3145736 | tf_op jit(solution)/shard_map/ppermute | solution.py:111
  105.9 9.4 %copy-start.2 = (s32[8]{0:T(128)S(1)}, s32[8]{0:T(128)}, u32[]{:S(2)}) copy-start(s32[8]{0:T(128)} %param.6) | copy-start | bytes 100
  143.0 34.1 %all-to-all-start.3 = ((bf16[32,32,512]{2,1,0:T(8,128)(2,1)}), bf16[32,32,512]{2,1,0:T(8,128)(2,1)S(1)}, u32[]{:S(2)}, u32[]{:S(2)}) async-start(bf16[32,32,512]{2,1,0:T(8,128)(2,1)} %bitcast.15), calls=%async_computation.4 | async-start | bytes 2097152 | tf_op jit(solution)/shard_map/all_to_all | solution.py:123
Sparse Core Ops, SparseCore 0:
  10.7 80.8 all-gather.2
Sparse Core Ops, SparseCore 1:
  115.4 45.9 reduce-scatter.1

commit v2 on v1

v2 whole, which is shorter than its diff:
```python
import functools

import jax
import jax.numpy as jnp
from jax import lax
from jax.experimental import pallas as pl
from jax.experimental.pallas import tpu as pltpu
from jax.sharding import Mesh, PartitionSpec as P


STEP_RATE = 0.25
ROW = ("z", "xl", "core")
BLOCK = 1024
PIECE = 32
WINDOW = 256
STATIC_HITS = 4
RING_ORDER = (4, 5, 3, 6, 2, 7, 1, 0)


def count_kernel(first_window, keys_ref, out_ref, hits_ref):
    window = first_window + pl.program_id(1)
    bag = keys_ref.shape[0]
    empty = jnp.full(keys_ref.shape[1:], -1, jnp.int32)
    hits = []
    total = jnp.zeros(keys_ref.shape[1:], jnp.int32)
    for k in range(bag):
        key = keys_ref[k]
        mine = (key >> 8) == window
        hits.append(empty)
        for j in range(k, 0, -1):
            hits[j] = jnp.where(mine, hits[j - 1], hits[j])
        hits[0] = jnp.where(mine, key & 255, hits[0])
        total = total + jnp.where(mine, 1, 0)
    for j in range(bag):
        hits_ref[j] = hits[j].astype(jnp.float32)
    most = jnp.max(total)
    rows = lax.broadcasted_iota(jnp.int32, (WINDOW, 128), 0).astype(jnp.bfloat16)
    one = jnp.ones((WINDOW, 128), jnp.bfloat16)
    zero = jnp.zeros((WINDOW, 128), jnp.bfloat16)

    def marks(j, d):
        wanted = jnp.broadcast_to(hits_ref[j, pl.ds(d, 1), :], (WINDOW, 128)).astype(jnp.bfloat16)
        return jnp.where(rows == wanted, one, zero)

    for d in range(keys_ref.shape[1]):
        counts = marks(0, d)
        for j in range(1, STATIC_HITS):
            counts = counts + marks(j, d)
        out_ref[:, d * 128 : (d + 1) * 128] = counts

    def more(j, carry):
        for d in range(keys_ref.shape[1]):
            out_ref[:, d * 128 : (d + 1) * 128] += marks(j, d)
        return carry

    lax.fori_loop(STATIC_HITS, most, more, 0)


def count_lookups(keys, first_row, rows):
    bag, owners, lanes = keys.shape
    groups = owners // 8
    return pl.pallas_call(
        functools.partial(count_kernel, first_row // WINDOW),
        grid=(groups, rows // WINDOW),
        in_specs=[pl.BlockSpec((bag, 8, lanes), lambda g, w: (0, g, 0))],
        out_specs=pl.BlockSpec((WINDOW, 8 * lanes), lambda g, w: (w, g)),
        out_shape=jax.ShapeDtypeStruct((rows, owners * lanes), jnp.bfloat16),
        scratch_shapes=[pltpu.VMEM((bag, 8, lanes), jnp.float32)],
        name="count_lookups",
    )(keys)


def pool_first_kernel(t0, t1, w_ref, out_ref):
    total = jnp.dot(t0[...], w_ref[0:BLOCK, :], preferred_element_type=jnp.float32)
    total += jnp.dot(t1[...], w_ref[BLOCK:, :], preferred_element_type=jnp.float32)
    for half in range(2):
        out_ref[half] = total[:, half * 128 : (half + 1) * 128]


def pool_first(t0, t1, counts):
    dim = t0.shape[0]
    samples = counts.shape[1]
    whole = pl.BlockSpec((dim, BLOCK), lambda n: (0, 0))
    return pl.pallas_call(
        pool_first_kernel,
        grid=(samples // 256,),
        in_specs=[whole] * 2 + [pl.BlockSpec((2 * BLOCK, 256), lambda n: (0, n))],
        out_specs=pl.BlockSpec((2, dim, 128), lambda n: (n, 0, 0)),
        out_shape=jax.ShapeDtypeStruct((samples // 128, dim, 128), jnp.float32),
        name="pool_first",
    )(t0, t1, counts)


def pool_rest_kernel(t0, t1, w_ref, first_ref, left_ref, right_ref):
    total = jnp.dot(t0[...], w_ref[0:BLOCK, :], preferred_element_type=jnp.float32)
    total += jnp.dot(t1[...], w_ref[BLOCK:, :], preferred_element_type=jnp.float32)
    left_ref[...] = total[:, :128] + first_ref[0]
    right_ref[...] = total[:, 128:] + first_ref[1]


def pool_rest(t0, t1, counts, first, pair):
    dim = t0.shape[0]
    whole = pl.BlockSpec((dim, BLOCK), lambda n: (0, 0))
    result = jax.ShapeDtypeStruct((dim, 128), jnp.float32)
    return pl.pallas_call(
        pool_rest_kernel,
        grid=(1,),
        in_specs=[whole] * 2
        + [pl.BlockSpec((2 * BLOCK, 256), lambda n: (0, pair)), pl.BlockSpec((2, dim, 128), lambda n: (pair, 0, 0))],
        out_specs=[pl.BlockSpec((dim, 128), lambda n: (0, 0))] * 2,
        out_shape=[result, result],
        name="pool_rest",
    )(t0, t1, counts, first)


def update_kernel(shift_ref, w0, w1, g0, g1, pieces_ref, out_ref):
    step = pl.program_id(0)
    gradient = jnp.dot(w0[...], g0[...], preferred_element_type=jnp.float32)
    gradient += jnp.dot(w1[...], g1[...], preferred_element_type=jnp.float32)
    for i in range(out_ref.shape[0]):
        old = pieces_ref[(8 * step + i - shift_ref[0]) & 31].astype(jnp.float32)
        out_ref[i] = (old - STEP_RATE * gradient[i * PIECE : (i + 1) * PIECE]).astype(jnp.bfloat16)


def update(shift, counts, grads, pieces):
    rows, samples = counts[0].shape
    dim = grads[0].shape[1]
    return pl.pallas_call(
        update_kernel,
        grid_spec=pltpu.PrefetchScalarGridSpec(
            num_scalar_prefetch=1,
            grid=(rows // 256,),
            in_specs=[pl.BlockSpec((256, samples), lambda n, s: (n, 0))] * 2
            + [pl.BlockSpec((samples, dim), lambda n, s: (0, 0))] * 2
            + [pl.BlockSpec(pieces.shape, lambda n, s: (0, 0, 0))],
            out_specs=pl.BlockSpec((8, PIECE, dim), lambda n, s: (n, 0, 0)),
        ),
        out_shape=jax.ShapeDtypeStruct(pieces.shape, jnp.bfloat16),
        name="update",
    )(shift, *counts, *grads, pieces)


def swap(values, axis):
    return lax.ppermute(values, axis, [(0, 1), (1, 0)])


def pass_on(values, by):
    return lax.ppermute(values, "z", [(i, (i + by) % 8) for i in range(8)])


def step(tables, indices, block_shift, pooled_grad):
    z, xl, core = (lax.axis_index(a) for a in ROW)
    quarter = 2 * xl + core
    shift = lax.dynamic_slice_in_dim(block_shift, lax.axis_index("grp"), 1)

    columns = lax.all_to_all(jnp.swapaxes(tables, 1, 2), "grp", 0, 0, tiled=True).reshape(-1, BLOCK)

    own = pooled_grad[:, 0, :]
    own = jnp.concatenate([own, swap(own, "xl")], axis=0)
    up, down = [own], [own]
    for hop in range(1, 5):
        up.append(pass_on(up[-1], 1))
        if hop < 4:
            down.append(pass_on(down[-1], -1))
    own_grads = jnp.concatenate(up + down[:0:-1], axis=0)
    other_grads = swap(own_grads, "core")

    ids = indices[:, 0, :].T.astype(jnp.int16)
    ids = lax.all_to_all(jnp.broadcast_to(ids, (8,) + ids.shape), "z", 0, 0, tiled=True)
    ids = lax.dynamic_slice_in_dim(jnp.concatenate([ids[::-1]] * 2, axis=0), 7 - z, 8)
    ids = ids[None]
    beside = swap(ids, "xl")
    ids_both = jnp.concatenate([ids, beside], axis=0)
    ids_other = swap(ids_both, "core")

    mine = ids[0].astype(jnp.int32)
    near = ((mine >> 10) & 3) ^ quarter
    pool_keys = jnp.where((mine >> 12) == z, (near << 10) | (mine & 1023), -1)
    pool_keys = jnp.stack([pool_keys[i] for i in RING_ORDER], axis=1)
    counts_near = count_lookups(pool_keys, 0, 2 * BLOCK)
    counts_far = count_lookups(pool_keys, 2 * BLOCK, 2 * BLOCK)
    across_core = swap(columns, "core")
    across_xl = swap(columns, "xl")
    across_both = swap(across_xl, "core")
    first = pool_first(columns, across_core, counts_near)
    sums = [None] * 8
    for pair in range(4):
        left, right = pool_rest(across_xl, across_both, counts_far, first, pair)
        sums[RING_ORDER[2 * pair]], sums[RING_ORDER[2 * pair + 1]] = left, right
    lower, upper = sums[4], sums[5]
    for hop in range(1, 5):
        lower = pass_on(lower, -1) + sums[4 - hop]
        if hop < 4:
            upper = pass_on(upper, 1)
            if hop < 3:
                upper = upper + sums[5 + hop]
    pooled = (lower + upper).T.astype(jnp.bfloat16)[:, None, :]

    pieces = lax.all_to_all(columns.T.reshape(32, PIECE, -1), ROW, 0, 0, tiled=True)
    counts = []
    for looked_up in (ids_both, ids_other):
        looked_up = looked_up.astype(jnp.int32).transpose(2, 1, 0, 3).reshape(32, 16, 128)
        place = ((looked_up >> 10) + shift[0]) & 31
        keys = jnp.where(((looked_up >> 5) & 31) == 4 * z + quarter, (place << 5) | (looked_up & 31), -1)
        counts.append(count_lookups(keys, 0, BLOCK))
    fresh = update(shift, counts, (own_grads, other_grads), pieces)
    updated = lax.all_to_all(fresh, ROW, 0, 0, tiled=True)
    return pooled, updated.reshape(1, BLOCK, -1)


def solution(mesh):
    split = Mesh(mesh.devices.reshape(8, 8, 2, 2), ("grp",) + ROW)
    return jax.shard_map(
        step,
        mesh=split,
        in_specs=(P(None, ROW, "grp"), P(ROW, "grp", None), P(), P(ROW, "grp", None)),
        out_specs=(P(ROW, "grp", None), P("grp", ROW, None)),
        check_vma=False,
    )
```

time: 189 us -> 209 us (1.11)
  starting transfers between devices: 27.9 us -> 56.7 us
  Pallas kernels: 34.2 us -> 58 us
  waiting for transfers between devices: 86.6 us -> 68.9 us
  between operations: 17.5 us -> 0.81 us
  local copies, waits for them, and re-layouts: 4.63 us -> 15.7 us
  matrix products: 10.1 us -> 0 us
  other arithmetic: 4.61 us -> 7.24 us
    all_to_all x4, waiting for transfers between devices: 38.8 us -> 6.33 us  [the longest x1 6.32 us: step(): lax.all_to_all(jnp.broadcast_to(ids, (8,) + ids.shape), 'z', 0, 0, tiled=...]
    ppermute x3 -> x21, waiting for transfers between devices: 33.2 us -> 62.5 us  [the longest x7 39.7 us: swap(): return lax.ppermute(values, axis, [(0, 1), (1, 0)])]
    ppermute x3 -> x21, starting transfers between devices: 2.13 us -> 31.1 us  [the longest x14 26.9 us: pass_on(): return lax.ppermute(values, 'z', [(i, (i + by) % 8) for i in range(8)])]
    pallas_call x3 -> x10, Pallas kernels: 34.2 us -> 58 us  [the longest x4 27.5 us: count_lookups(): pl.pallas_call(functools.partial(count_kernel, first_row // WINDOW), grid...]
    reduce_scatter x1 -> x0, waiting for transfers between devices: 13.9 us -> none  [per_device(): pooled = lax.psum_scatter(partial, 'z', scatter_dimension=0, tiled=True)[0]]
    dot_general x1 -> x0, matrix products: 10.1 us -> none  [per_device(): gradient = jnp.dot(update_counts, grads, preferred_element_type=jnp.float32)]
    unnamed x8 -> x26, local copies, waits for them, and re-layouts: 1.75 us -> 9.67 us
    add x0 -> x5, other arithmetic: none -> 2.99 us  [the longest x3 2.93 us: step(): lower = pass_on(lower, -1) + sums[4 - hop]]
  transfers between devices with their start and end apart: 9 -> 25, of which waited for: 5 -> 11; matrix products, arithmetic and copies ran while one was open for 10% -> 9% of each run, Pallas kernels for 18% -> 28%
where the time goes in v2:
time: 209 us; the launch traced here: 207 us
  waiting for transfers between devices  68.9 us (33%)
  Pallas kernels  58 us (28%)
  starting transfers between devices  56.7 us (27%)
  local copies, waits for them, and re-layouts  15.7 us (8%)
  other arithmetic  7.24 us (3%)
    ppermute x7, waiting for transfers between devices, swap(): return lax.ppermute(values, axis, [(0, 1), (1, 0)])  39.7 us
    pallas_call x4, Pallas kernels, count_lookups(): pl.pallas_call(functools.partial(count_kernel, first_row // WINDOW), grid...  27.5 us
    ppermute x14, starting transfers between devices, pass_on(): return lax.ppermute(values, 'z', [(i, (i + by) % 8) for i in range(8)])  26.9 us
    ppermute x14, waiting for transfers between devices, pass_on(): return lax.ppermute(values, 'z', [(i, (i + by) % 8) for i in range(8)])  22.8 us
    pallas_call x4, Pallas kernels, pool_rest(): pl.pallas_call(pool_rest_kernel, grid=(1,), in_specs=[whole] * 2 + [pl.Bl...  14.1 us
    pallas_call x1, Pallas kernels, update(): pl.pallas_call(update_kernel, grid_spec=pltpu.PrefetchScalarGridSpec(num_...  10.1 us
    unnamed x26, local copies, waits for them, and re-layouts  9.67 us
    all_to_all x1, starting transfers between devices, step(): lax.all_to_all(jnp.swapaxes(tables, 1, 2), 'grp', 0, 0, tiled=True)  7.43 us
  transfers between devices with their start and end apart: 25, of which 11 were waited for; matrix products, arithmetic and copies ran while one was open for 9% of the time, Pallas kernels for 28%

profile of v2, /device:TPU:4, one launch (start us, length us, event | category | flops | bytes accessed | tf_op | source)
XLA Modules:
  0.0 207.3 jit_solution(15316025325943758607)
XLA Ops:
  1.9 4.2 %collective-permute-done.12 = bf16[128,512]{1,0:T(8,128)(2,1)S(1)} collective-permute-done((bf16[128,512]{1,0:T(8,128)(2,1)}, bf16[128,512]{1,0:T(8,128)(2,1)S(1)}, u32[]{:S(2)}, u32[]{:S(2)}) %collective-permute-start.12) | collective-permute-done | bytes 131104 | tf_op jit(solution)/shard_map/ppermute | solution.py:144
  9.1 4.0 %collective-permute-start.17 = (bf16[256,512]{1,0:T(8,128)(2,1)S(1)}, bf16[256,512]{1,0:T(8,128)(2,1)S(1)}, u32[]{:S(2)}, u32[]{:S(2)}) collective-permute-start(bf16[256,512]{1,0:T(8,128)(2,1)S(1)} %pad_maximum_fusion), channel_id=1, source_target_pairs={{0,28},{4,0},{8,4},{12,8},{16,12},{20,16},{24,20},{28,24},{1,29},{... | collective-permute-start | bytes 786440 | tf_op jit(solution)/shard_map/ppermute | solution.py:148
  13.1 5.4 %collective-permute-done.13 = bf16[256,512]{1,0:T(8,128)(2,1)S(1)} collective-permute-done((bf16[256,512]{1,0:T(8,128)(2,1)S(1)}, bf16[256,512]{1,0:T(8,128)(2,1)S(1)}, u32[]{:S(2)}, u32[]{:S(2)}) %collective-permute-start.13) | collective-permute-done | bytes 262176 | tf_op jit(solution)/shard_map/ppermute | solution.py:148
  18.5 7.4 %all-to-all-start = ((bf16[8,64,1024]{2,1,0:T(8,128)(2,1)}), bf16[8,64,1024]{2,1,0:T(8,128)(2,1)S(1)}, u32[]{:S(2)}, u32[]{:S(2)}) async-start(bf16[8,64,1024]{2,1,0:T(8,128)(2,1)} %bitcast.53), calls=%async_computation | async-start | bytes 2097152 | tf_op jit(solution)/shard_map/all_to_all | solution.py:156
  26.6 3.2 %collective-permute-start.18 = (bf16[256,512]{1,0:T(8,128)(2,1)S(1)}, bf16[256,512]{1,0:T(8,128)(2,1)S(1)}, u32[]{:S(2)}, u32[]{:S(2)}) collective-permute-start(bf16[256,512]{1,0:T(8,128)(2,1)S(1)} %collective-permute-done.17), channel_id=1, source_target_pairs={{0,28},{4,0},{8,4},{12,8},{16,12},{20,16},{24,20},{28,24},{1,29},{... | collective-permute-start | bytes 786440 | tf_op jit(solution)/shard_map/ppermute | solution.py:148
  30.5 6.9 %collective-permute-done.15 = bf16[256,512]{1,0:T(8,128)(2,1)S(1)} collective-permute-done((bf16[256,512]{1,0:T(8,128)(2,1)S(1)}, bf16[256,512]{1,0:T(8,128)(2,1)S(1)}, u32[]{:S(2)}, u32[]{:S(2)}) %collective-permute-start.15) | collective-permute-done | bytes 262176 | tf_op jit(solution)/shard_map/ppermute | solution.py:148
  47.9 6.2 %all-to-all-start.1 = ((s16[8,32,128]{2,1,0:T(8,128)(2,1)}), s16[8,32,128]{2,1,0:T(8,128)(2,1)S(1)}, u32[]{:S(2)}, u32[]{:S(2)}) async-start(s16[8,32,128]{2,1,0:T(8,128)(2,1)} %broadcast_in_dim.18), calls=%async_computation.1 | async-start | bytes 131072 | tf_op jit(solution)/shard_map/all_to_all | solution.py:169
  56.1 6.3 %all-to-all-done.1 = s16[8,32,128]{2,1,0:T(8,128)(2,1)S(1)} async-done(((s16[8,32,128]{2,1,0:T(8,128)(2,1)}), s16[8,32,128]{2,1,0:T(8,128)(2,1)S(1)}, u32[]{:S(2)}, u32[]{:S(2)}) %all-to-all-start.1) | async-done | bytes 65568 | tf_op jit(solution)/shard_map/all_to_all | solution.py:169
  62.4 4.7 %all-to-all-start.2 = ((bf16[32,32,512]{2,1,0:T(8,128)(2,1)}), bf16[32,32,512]{2,1,0:T(8,128)(2,1)}, u32[]{:S(2)}, u32[]{:S(2)}) async-start(bf16[32,32,512]{2,1,0:T(8,128)(2,1)} %bitcast.29), calls=%async_computation.2 | async-start | bytes 2097152 | tf_op jit(solution)/shard_map/all_to_all | solution.py:199
  69.4 35.5 %collective-permute-done.10 = s16[1,8,32,128]{3,2,1,0:T(8,128)(2,1)S(1)} collective-permute-done((s16[1,8,32,128]{3,2,1,0:T(8,128)(2,1)S(1)}, s16[1,8,32,128]{3,2,1,0:T(8,128)(2,1)S(1)}, u32[]{:S(2)}, u32[]{:S(2)}) %collective-permute-start.10) | collective-permute-done | bytes 65568 | tf_op jit(solution)/shard_map/ppermute | solution.py:144
  108.6 7.0 %count_lookups.6.w0 = bf16[1024,2048]{1,0:T(8,128)(2,1)} custom-call(s32[32,16,128]{2,1,0:T(8,128)} %bitcast.51), custom_call_target="tpu_custom_call" | custom-call | tf_op jit(solution)/shard_map/count_lookups/pallas_call | solution.py:62
  117.3 7.1 %count_lookups.7.w1 = bf16[1024,2048]{1,0:T(8,128)(2,1)} custom-call(s32[32,16,128]{2,1,0:T(8,128)} %bitcast.52), custom_call_target="tpu_custom_call" | custom-call | tf_op jit(solution)/shard_map/count_lookups/pallas_call | solution.py:62
  124.3 10.1 %update.1 = bf16[32,32,512]{2,1,0:T(8,128)(2,1)} custom-call(s32[1]{0:T(128)} %dynamic_slice.7.shift_ref, bf16[1024,2048]{1,0:T(8,128)(2,1)} %count_lookups.6.w0, bf16[1024,2048]{1,0:T(8,128)(2,1)} %count_lookups.7.w1, bf16[2048,512]{1,0:T(8,128)(2,1)} %constant_dynamic-update-slice_fusion.g0, bf16[2048,512]{1,0:T(8,128)(2,1)} %collective-permute-done.20.g1, ...), custom_call_target="tpu_custom_call" | custom-call | tf_op jit(solution)/shard_map/update/pallas_call | solution.py:128
  134.4 7.3 %all-to-all-start.3 = ((bf16[32,32,512]{2,1,0:T(8,128)(2,1)}), bf16[32,32,512]{2,1,0:T(8,128)(2,1)}, u32[]{:S(2)}, u32[]{:S(2)}) async-start(bf16[32,32,512]{2,1,0:T(8,128)(2,1)} %update.1), calls=%async_computation.3 | async-start | bytes 2097152 | tf_op jit(solution)/shard_map/all_to_all | solution.py:207
  142.7 6.7 %count_lookups.4.w_ref = bf16[2048,1024]{1,0:T(8,128)(2,1)} custom-call(s32[32,8,128]{2,1,0:T(8,128)} %stack.3.keys_ref), custom_call_target="tpu_custom_call" | custom-call | tf_op jit(solution)/shard_map/count_lookups/pallas_call | solution.py:62
  149.3 6.7 %count_lookups.5.w_ref = bf16[2048,1024]{1,0:T(8,128)(2,1)} custom-call(s32[32,8,128]{2,1,0:T(8,128)} %stack.3.keys_ref), custom_call_target="tpu_custom_call" | custom-call | tf_op jit(solution)/shard_map/count_lookups/pallas_call | solution.py:62
  156.0 6.4 %pool_first.1.first_ref = f32[8,512,128]{2,1,0:T(8,128)} custom-call(bf16[512,1024]{1,0:T(8,128)(2,1)} %bitcast.50, bf16[512,1024]{1,0:T(8,128)(2,1)} %collective-permute-done.2.t1, bf16[2048,1024]{1,0:T(8,128)(2,1)} %count_lookups.5.w_ref), custom_call_target="tpu_custom_call" | custom-call | tf_op jit(solution)/shard_map/pool_first/pallas_call | solution.py:84
  163.4 3.5 %pool_rest.4 = (f32[512,128]{1,0:T(8,128)}, f32[512,128]{1,0:T(8,128)}) custom-call(bf16[512,1024]{1,0:T(8,128)(2,1)} %copy-done, bf16[512,1024]{1,0:T(8,128)(2,1)} %copy-done.1, bf16[2048,1024]{1,0:T(8,128)(2,1)} %count_lookups.4.w_ref, f32[8,512,128]{2,1,0:T(8,128)} %pool_first.1.first_ref), custom_call_target="tpu_custom_call" | custom-call | tf_op jit(solution)/shard_map/pool_rest/pallas_call | solution.py:105
  169.9 3.5 %pool_rest.5 = (f32[512,128]{1,0:T(8,128)}, f32[512,128]{1,0:T(8,128)}) custom-call(bf16[512,1024]{1,0:T(8,128)(2,1)} %copy-done, bf16[512,1024]{1,0:T(8,128)(2,1)} %copy-done.1, bf16[2048,1024]{1,0:T(8,128)(2,1)} %count_lookups.4.w_ref, f32[8,512,128]{2,1,0:T(8,128)} %pool_first.1.first_ref), custom_call_target="tpu_custom_call" | custom-call | tf_op jit(solution)/shard_map/pool_rest/pallas_call | solution.py:105
  177.1 3.7 %collective-permute-start.4 = (f32[512,128]{1,0:T(8,128)S(1)}, f32[512,128]{1,0:T(8,128)S(1)}, u32[]{:S(2)}, u32[]{:S(2)}) collective-permute-start(f32[512,128]{1,0:T(8,128)S(1)} %add.51), channel_id=1, source_target_pairs={{0,28},{4,0},{8,4},{12,8},{16,12},{20,16},{24,20},{28,24},{1,29},{... | collective-permute-start | bytes 786440 | tf_op jit(solution)/shard_map/ppermute | solution.py:148
  180.8 3.5 %pool_rest.6 = (f32[512,128]{1,0:T(8,128)}, f32[512,128]{1,0:T(8,128)}) custom-call(bf16[512,1024]{1,0:T(8,128)(2,1)} %copy-done, bf16[512,1024]{1,0:T(8,128)(2,1)} %copy-done.1, bf16[2048,1024]{1,0:T(8,128)(2,1)} %count_lookups.4.w_ref, f32[8,512,128]{2,1,0:T(8,128)} %pool_first.1.first_ref), custom_call_target="tpu_custom_call" | custom-call | tf_op jit(solution)/shard_map/pool_rest/pallas_call | solution.py:105
  186.7 3.8 %collective-permute-start.5 = (f32[512,128]{1,0:T(8,128)S(1)}, f32[512,128]{1,0:T(8,128)S(1)}, u32[]{:S(2)}, u32[]{:S(2)}) collective-permute-start(f32[512,128]{1,0:T(8,128)S(1)} %add.52), channel_id=1, source_target_pairs={{0,28},{4,0},{8,4},{12,8},{16,12},{20,16},{24,20},{28,24},{1,29},{... | collective-permute-start | bytes 786440 | tf_op jit(solution)/shard_map/ppermute | solution.py:148
  190.5 3.5 %pool_rest.7 = (f32[512,128]{1,0:T(8,128)}, f32[512,128]{1,0:T(8,128)}) custom-call(bf16[512,1024]{1,0:T(8,128)(2,1)} %copy-done, bf16[512,1024]{1,0:T(8,128)(2,1)} %copy-done.1, bf16[2048,1024]{1,0:T(8,128)(2,1)} %count_lookups.4.w_ref, f32[8,512,128]{2,1,0:T(8,128)} %pool_first.1.first_ref), custom_call_target="tpu_custom_call" | custom-call | tf_op jit(solution)/shard_map/pool_rest/pallas_call | solution.py:105
  195.6 3.8 %collective-permute-start.6 = (f32[512,128]{1,0:T(8,128)S(1)}, f32[512,128]{1,0:T(8,128)S(1)}, u32[]{:S(2)}, u32[]{:S(2)}) collective-permute-start(f32[512,128]{1,0:T(8,128)S(1)} %add.53), channel_id=1, source_target_pairs={{0,28},{4,0},{8,4},{12,8},{16,12},{20,16},{24,20},{28,24},{1,29},{... | collective-permute-start | bytes 786440 | tf_op jit(solution)/shard_map/ppermute | solution.py:148
  (84 shorter events, 46.2 us)
Async XLA Ops:
  7.1 11.4 %collective-permute-start.13 = (bf16[256,512]{1,0:T(8,128)(2,1)S(1)}, bf16[256,512]{1,0:T(8,128)(2,1)S(1)}, u32[]{:S(2)}, u32[]{:S(2)}) collective-permute-start(bf16[256,512]{1,0:T(8,128)(2,1)S(1)} %pad_maximum_fusion), channel_id=1, source_target_pairs={{0,4},{4,8},{8,12},{12,16},{16,20},{20,24},{24,28},{28,0},{1,5},{5... | collective-permute-start | bytes 786440 | tf_op jit(solution)/shard_map/ppermute | solution.py:148
  9.1 17.5 %collective-permute-start.17 = (bf16[256,512]{1,0:T(8,128)(2,1)S(1)}, bf16[256,512]{1,0:T(8,128)(2,1)S(1)}, u32[]{:S(2)}, u32[]{:S(2)}) collective-permute-start(bf16[256,512]{1,0:T(8,128)(2,1)S(1)} %pad_maximum_fusion), channel_id=1, source_target_pairs={{0,28},{4,0},{8,4},{12,8},{16,12},{20,16},{24,20},{28,24},{1,29},{... | collective-permute-start | bytes 786440 | tf_op jit(solution)/shard_map/ppermute | solution.py:148
  18.5 11.3 %collective-permute-start.14 = (bf16[256,512]{1,0:T(8,128)(2,1)S(1)}, bf16[256,512]{1,0:T(8,128)(2,1)S(1)}, u32[]{:S(2)}, u32[]{:S(2)}) collective-permute-start(bf16[256,512]{1,0:T(8,128)(2,1)S(1)} %collective-permute-done.13), channel_id=1, source_target_pairs={{0,4},{4,8},{8,12},{12,16},{16,20},{20,24},{24,28},{28,0},{1,5},{5... | collective-permute-start | bytes 786440 | tf_op jit(solution)/shard_map/ppermute | solution.py:148
  18.5 28.7 %all-to-all-start = ((bf16[8,64,1024]{2,1,0:T(8,128)(2,1)}), bf16[8,64,1024]{2,1,0:T(8,128)(2,1)S(1)}, u32[]{:S(2)}, u32[]{:S(2)}) async-start(bf16[8,64,1024]{2,1,0:T(8,128)(2,1)} %bitcast.53), calls=%async_computation | async-start | bytes 2097152 | tf_op jit(solution)/shard_map/all_to_all | solution.py:156
  26.6 11.5 %collective-permute-start.18 = (bf16[256,512]{1,0:T(8,128)(2,1)S(1)}, bf16[256,512]{1,0:T(8,128)(2,1)S(1)}, u32[]{:S(2)}, u32[]{:S(2)}) collective-permute-start(bf16[256,512]{1,0:T(8,128)(2,1)S(1)} %collective-permute-done.17), channel_id=1, source_target_pairs={{0,28},{4,0},{8,4},{12,8},{16,12},{20,16},{24,20},{28,24},{1,29},{... | collective-permute-start | bytes 786440 | tf_op jit(solution)/shard_map/ppermute | solution.py:148
  29.8 7.6 %collective-permute-start.15 = (bf16[256,512]{1,0:T(8,128)(2,1)S(1)}, bf16[256,512]{1,0:T(8,128)(2,1)S(1)}, u32[]{:S(2)}, u32[]{:S(2)}) collective-permute-start(bf16[256,512]{1,0:T(8,128)(2,1)S(1)} %collective-permute-done.14), channel_id=1, source_target_pairs={{0,4},{4,8},{8,12},{12,16},{16,20},{20,24},{24,28},{28,0},{1,5},{5... | collective-permute-start | bytes 786440 | tf_op jit(solution)/shard_map/ppermute | solution.py:148
  37.4 7.6 %collective-permute-start.16 = (bf16[256,512]{1,0:T(8,128)(2,1)S(1)}, bf16[256,512]{1,0:T(8,128)(2,1)S(1)}, u32[]{:S(2)}, u32[]{:S(2)}) collective-permute-start(bf16[256,512]{1,0:T(8,128)(2,1)S(1)} %collective-permute-done.15), channel_id=1, source_target_pairs={{0,4},{4,8},{8,12},{12,16},{16,20},{20,24},{24,28},{28,0},{1,5},{5... | collective-permute-start | bytes 786440 | tf_op jit(solution)/shard_map/ppermute | solution.py:148
  38.1 7.6 %collective-permute-start.19 = (bf16[256,512]{1,0:T(8,128)(2,1)S(1)}, bf16[256,512]{1,0:T(8,128)(2,1)S(1)}, u32[]{:S(2)}, u32[]{:S(2)}) collective-permute-start(bf16[256,512]{1,0:T(8,128)(2,1)S(1)} %collective-permute-done.18), channel_id=1, source_target_pairs={{0,28},{4,0},{8,4},{12,8},{16,12},{20,16},{24,20},{28,24},{1,29},{... | collective-permute-start | bytes 786440 | tf_op jit(solution)/shard_map/ppermute | solution.py:148
  47.9 14.6 %all-to-all-start.1 = ((s16[8,32,128]{2,1,0:T(8,128)(2,1)}), s16[8,32,128]{2,1,0:T(8,128)(2,1)S(1)}, u32[]{:S(2)}, u32[]{:S(2)}) async-start(s16[8,32,128]{2,1,0:T(8,128)(2,1)} %broadcast_in_dim.18), calls=%async_computation.1 | async-start | bytes 131072 | tf_op jit(solution)/shard_map/all_to_all | solution.py:169
  54.8 69.6 %collective-permute-start.20 = (bf16[2048,512]{1,0:T(8,128)(2,1)}, bf16[2048,512]{1,0:T(8,128)(2,1)}, u32[]{:S(2)}, u32[]{:S(2)}) collective-permute-start(bf16[2048,512]{1,0:T(8,128)(2,1)} %constant_dynamic-update-slice_fusion.g0), channel_id=1, source_target_pairs={{0,1},{1,0},{2,3},{3,2},{4,5},{5,4},{6,7},{7,6},{8,9},{9,8},{10,11... | collective-permute-start | bytes 6291464 | tf_op jit(solution)/shard_map/ppermute | solution.py:144
  62.4 61.9 %all-to-all-start.2 = ((bf16[32,32,512]{2,1,0:T(8,128)(2,1)}), bf16[32,32,512]{2,1,0:T(8,128)(2,1)}, u32[]{:S(2)}, u32[]{:S(2)}) async-start(bf16[32,32,512]{2,1,0:T(8,128)(2,1)} %bitcast.29), calls=%async_computation.2 | async-start | bytes 2097152 | tf_op jit(solution)/shard_map/all_to_all | solution.py:199
  67.1 39.5 %collective-permute-start = (bf16[512,1024]{1,0:T(8,128)(2,1)S(1)}, bf16[512,1024]{1,0:T(8,128)(2,1)S(1)}, u32[]{:S(2)}, u32[]{:S(2)}) collective-permute-start(bf16[512,1024]{1,0:T(8,128)(2,1)S(1)} %bitcast.48), channel_id=1, source_target_pairs={{0,2},{2,0},{1,3},{3,1},{4,6},{6,4},{5,7},{7,5},{8,10},{10,8},{9,1... | collective-permute-start | bytes 3145736 | tf_op jit(solution)/shard_map/ppermute | solution.py:144
  68.9 36.0 %collective-permute-start.10 = (s16[1,8,32,128]{3,2,1,0:T(8,128)(2,1)S(1)}, s16[1,8,32,128]{3,2,1,0:T(8,128)(2,1)S(1)}, u32[]{:S(2)}, u32[]{:S(2)}) collective-permute-start(s16[1,8,32,128]{3,2,1,0:T(8,128)(2,1)S(1)} %fusion.24), channel_id=1, source_target_pairs={{0,2},{2,0},{1,3},{3,1},{4,6},{6,4},{5,7},{7,5},{8,10},{10,8},{9,1... | collective-permute-start | bytes 196616 | tf_op jit(solution)/shard_map/ppermute | solution.py:144
  105.5 10.1 %collective-permute-start.11 = (s16[2,8,32,128]{3,2,1,0:T(8,128)(2,1)}, s16[2,8,32,128]{3,2,1,0:T(8,128)(2,1)S(1)}, u32[]{:S(2)}, u32[]{:S(2)}) collective-permute-start(s16[2,8,32,128]{3,2,1,0:T(8,128)(2,1)} %pad_add_fusion), channel_id=1, source_target_pairs={{0,1},{1,0},{2,3},{3,2},{4,5},{5,4},{6,7},{7,6},{8,9},{9,8},{10,11... | collective-permute-start | bytes 393224 | tf_op jit(solution)/shard_map/ppermute | solution.py:144
  106.1 49.9 %collective-permute-start.2 = (bf16[512,1024]{1,0:T(8,128)(2,1)S(1)}, bf16[512,1024]{1,0:T(8,128)(2,1)}, u32[]{:S(2)}, u32[]{:S(2)}) collective-permute-start(bf16[512,1024]{1,0:T(8,128)(2,1)S(1)} %bitcast.49), channel_id=1, source_target_pairs={{0,1},{1,0},{2,3},{3,2},{4,5},{5,4},{6,7},{7,6},{8,9},{9,8},{10,11... | collective-permute-start | bytes 3145736 | tf_op jit(solution)/shard_map/ppermute | solution.py:144
  106.6 55.8 %collective-permute-start.1 = (bf16[512,1024]{1,0:T(8,128)(2,1)S(1)}, bf16[512,1024]{1,0:T(8,128)(2,1)S(1)}, u32[]{:S(2)}, u32[]{:S(2)}) collective-permute-start(bf16[512,1024]{1,0:T(8,128)(2,1)S(1)} %collective-permute-done.t0), channel_id=1, source_target_pairs={{0,1},{1,0},{2,3},{3,2},{4,5},{5,4},{6,7},{7,6},{8,9},{9,8},{10,11... | collective-permute-start | bytes 3145736 | tf_op jit(solution)/shard_map/ppermute | solution.py:144
  134.4 70.6 %all-to-all-start.3 = ((bf16[32,32,512]{2,1,0:T(8,128)(2,1)}), bf16[32,32,512]{2,1,0:T(8,128)(2,1)}, u32[]{:S(2)}, u32[]{:S(2)}) async-start(bf16[32,32,512]{2,1,0:T(8,128)(2,1)} %update.1), calls=%async_computation.3 | async-start | bytes 2097152 | tf_op jit(solution)/shard_map/all_to_all | solution.py:207
  166.9 9.2 %collective-permute-start.3 = (f32[512,128]{1,0:T(8,128)}, f32[512,128]{1,0:T(8,128)S(1)}, u32[]{:S(2)}, u32[]{:S(2)}) collective-permute-start(f32[512,128]{1,0:T(8,128)} %get-tuple-element.10), channel_id=1, source_target_pairs={{0,28},{4,0},{8,4},{12,8},{16,12},{20,16},{24,20},{28,24},{1,29},{... | collective-permute-start | bytes 786440 | tf_op jit(solution)/shard_map/ppermute | solution.py:148
  169.9 14.4 %collective-permute-start.7 = (f32[512,128]{1,0:T(8,128)}, f32[512,128]{1,0:T(8,128)S(1)}, u32[]{:S(2)}, u32[]{:S(2)}) collective-permute-start(f32[512,128]{1,0:T(8,128)} %get-tuple-element.15), channel_id=1, source_target_pairs={{0,4},{4,8},{8,12},{12,16},{16,20},{20,24},{24,28},{28,0},{1,5},{5... | collective-permute-start | bytes 786440 | tf_op jit(solution)/shard_map/ppermute | solution.py:148
  177.1 8.7 %collective-permute-start.4 = (f32[512,128]{1,0:T(8,128)S(1)}, f32[512,128]{1,0:T(8,128)S(1)}, u32[]{:S(2)}, u32[]{:S(2)}) collective-permute-start(f32[512,128]{1,0:T(8,128)S(1)} %add.51), channel_id=1, source_target_pairs={{0,28},{4,0},{8,4},{12,8},{16,12},{20,16},{24,20},{28,24},{1,29},{... | collective-permute-start | bytes 786440 | tf_op jit(solution)/shard_map/ppermute | solution.py:148
  184.3 9.7 %collective-permute-start.8 = (f32[512,128]{1,0:T(8,128)S(1)}, f32[512,128]{1,0:T(8,128)S(1)}, u32[]{:S(2)}, u32[]{:S(2)}) collective-permute-start(f32[512,128]{1,0:T(8,128)S(1)} %add.55), channel_id=1, source_target_pairs={{0,4},{4,8},{8,12},{12,16},{16,20},{20,24},{24,28},{28,0},{1,5},{5... | collective-permute-start | bytes 786440 | tf_op jit(solution)/shard_map/ppermute | solution.py:148
  186.7 7.9 %collective-permute-start.5 = (f32[512,128]{1,0:T(8,128)S(1)}, f32[512,128]{1,0:T(8,128)S(1)}, u32[]{:S(2)}, u32[]{:S(2)}) collective-permute-start(f32[512,128]{1,0:T(8,128)S(1)} %add.52), channel_id=1, source_target_pairs={{0,28},{4,0},{8,4},{12,8},{16,12},{20,16},{24,20},{28,24},{1,29},{... | collective-permute-start | bytes 786440 | tf_op jit(solution)/shard_map/ppermute | solution.py:148
  194.1 7.7 %collective-permute-start.9 = (f32[512,128]{1,0:T(8,128)S(1)}, f32[512,128]{1,0:T(8,128)S(1)}, u32[]{:S(2)}, u32[]{:S(2)}) collective-permute-start(f32[512,128]{1,0:T(8,128)S(1)} %add.56), channel_id=1, source_target_pairs={{0,4},{4,8},{8,12},{12,16},{16,20},{20,24},{24,28},{28,0},{1,5},{5... | collective-permute-start | bytes 786440 | tf_op jit(solution)/shard_map/ppermute | solution.py:148
  195.6 7.7 %collective-permute-start.6 = (f32[512,128]{1,0:T(8,128)S(1)}, f32[512,128]{1,0:T(8,128)S(1)}, u32[]{:S(2)}, u32[]{:S(2)}) collective-permute-start(f32[512,128]{1,0:T(8,128)S(1)} %add.53), channel_id=1, source_target_pairs={{0,28},{4,0},{8,4},{12,8},{16,12},{20,16},{24,20},{28,24},{1,29},{... | collective-permute-start | bytes 786440 | tf_op jit(solution)/shard_map/ppermute | solution.py:148
  (9 other events, 194.2 us)

commit v3 on v1

v3 whole, which is shorter than its diff:
```python
import jax
import jax.numpy as jnp
from jax import lax
from jax.experimental import pallas as pl
from jax.experimental.pallas import tpu as pltpu
from jax.sharding import Mesh, PartitionSpec as P


STEP_RATE = 0.25
ROW = ("z", "xl", "core")
BLOCK = 1024
PIECE = 32
WINDOW = 256
STATIC_HITS = 4


def count_kernel(keys_ref, out_ref, hits_ref):
    windows = out_ref.shape[1] // WINDOW
    bag, owners, lanes = keys_ref.shape
    most = jnp.zeros((owners, lanes), jnp.int32)
    for w in range(windows):
        window = pl.program_id(1) * windows + w
        hits = []
        total = jnp.zeros((owners, lanes), jnp.int32)
        for k in range(bag):
            key = keys_ref[k]
            mine = (key >> 8) == window
            hits.append(jnp.full((owners, lanes), -1, jnp.int32))
            for j in range(k, 0, -1):
                hits[j] = jnp.where(mine, hits[j - 1], hits[j])
            hits[0] = jnp.where(mine, key & 255, hits[0])
            total = total + jnp.where(mine, 1, 0)
        for j in range(bag):
            hits_ref[w, j] = hits[j].astype(jnp.float32)
        most = jnp.maximum(most, total)
    rows = lax.broadcasted_iota(jnp.int32, (WINDOW, lanes), 0).astype(jnp.bfloat16)
    one = jnp.ones((WINDOW, lanes), jnp.bfloat16)
    zero = jnp.zeros((WINDOW, lanes), jnp.bfloat16)

    def marks(w, j, d):
        wanted = jnp.broadcast_to(hits_ref[w, j, pl.ds(d, 1), :], (WINDOW, lanes)).astype(jnp.bfloat16)
        return jnp.where(rows == wanted, one, zero)

    def place(w, d):
        return d, pl.ds(w * WINDOW, WINDOW)

    for w in range(windows):
        for d in range(owners):
            counts = marks(w, 0, d)
            for j in range(1, STATIC_HITS):
                counts = counts + marks(w, j, d)
            out_ref[place(w, d)] = counts

    def more(j, carry):
        for w in range(windows):
            for d in range(owners):
                out_ref[place(w, d)] += marks(w, j, d)
        return carry

    lax.fori_loop(STATIC_HITS, jnp.max(most), more, 0)


def count_lookups(keys, rows):
    bag, owners, lanes = keys.shape
    return pl.pallas_call(
        count_kernel,
        grid=(owners // 8, rows // BLOCK),
        in_specs=[pl.BlockSpec((bag, 8, lanes), lambda g, w: (0, g, 0))],
        out_specs=pl.BlockSpec((8, BLOCK, lanes), lambda g, w: (g, w, 0)),
        out_shape=jax.ShapeDtypeStruct((owners, rows, lanes), jnp.bfloat16),
        scratch_shapes=[pltpu.VMEM((BLOCK // WINDOW, bag, 8, lanes), jnp.float32)],
        name="count",
    )(keys)


def side_by_side(w_ref, rows=slice(None)):
    return jnp.concatenate([w_ref[i, rows] for i in range(w_ref.shape[0])], axis=1)


def pool_kernel(t0, t1, t2, t3, w_ref, out_ref):
    total = jnp.dot(t0[...], side_by_side(w_ref, slice(0, BLOCK)), preferred_element_type=jnp.float32)
    for q, t in enumerate((t1, t2, t3), 1):
        rows = slice(q * BLOCK, (q + 1) * BLOCK)
        total += jnp.dot(t[...], side_by_side(w_ref, rows), preferred_element_type=jnp.float32)
    for half in range(2):
        out_ref[half] = total[:, half * 128 : (half + 1) * 128]


def pool(tables, counts):
    dim = tables[0].shape[0]
    owners, rows, lanes = counts.shape
    return pl.pallas_call(
        pool_kernel,
        grid=(owners // 2,),
        in_specs=[pl.BlockSpec((dim, BLOCK), lambda n: (0, 0))] * 4
        + [pl.BlockSpec((2, rows, lanes), lambda n: (n, 0, 0))],
        out_specs=pl.BlockSpec((2, dim, lanes), lambda n: (n, 0, 0)),
        out_shape=jax.ShapeDtypeStruct((owners, dim, lanes), jnp.float32),
        name="pool",
    )(*tables, counts)


def update_kernel(shift_ref, w_ref, grads_ref, pieces_ref, out_ref):
    step = pl.program_id(0)
    gradient = jnp.dot(side_by_side(w_ref), grads_ref[...], preferred_element_type=jnp.float32)
    for i in range(out_ref.shape[0]):
        old = pieces_ref[(8 * step + i - shift_ref[0]) & 31].astype(jnp.float32)
        out_ref[i] = (old - STEP_RATE * gradient[i * PIECE : (i + 1) * PIECE]).astype(jnp.bfloat16)


def update(shift, counts, grads, pieces):
    owners, rows, lanes = counts.shape
    samples, dim = grads.shape
    return pl.pallas_call(
        update_kernel,
        grid_spec=pltpu.PrefetchScalarGridSpec(
            num_scalar_prefetch=1,
            grid=(rows // 256,),
            in_specs=[
                pl.BlockSpec((owners, 256, lanes), lambda n, s: (0, n, 0)),
                pl.BlockSpec((samples, dim), lambda n, s: (0, 0)),
                pl.BlockSpec(pieces.shape, lambda n, s: (0, 0, 0)),
            ],
            out_specs=pl.BlockSpec((8, PIECE, dim), lambda n, s: (n, 0, 0)),
        ),
        out_shape=jax.ShapeDtypeStruct(pieces.shape, jnp.bfloat16),
        name="update",
    )(shift, counts, grads, pieces)


def swap(values, axis):
    return lax.ppermute(values, axis, [(0, 1), (1, 0)])


def step(tables, indices, block_shift, pooled_grad):
    z, xl, core = (lax.axis_index(a) for a in ROW)
    quarter = 2 * xl + core
    shift = lax.dynamic_slice_in_dim(block_shift, lax.axis_index("grp"), 1)

    own = pooled_grad[:, 0, :]
    own = jnp.concatenate([own, swap(own, "xl")], axis=0)
    grads = lax.all_gather(own, ("z", "core"), axis=0, tiled=True)

    columns = lax.all_to_all(jnp.swapaxes(tables, 1, 2), "grp", 0, 0, tiled=True).reshape(-1, BLOCK)

    ids = indices[:, 0, :].T.astype(jnp.int16)[None]
    ids = jnp.concatenate([ids, swap(ids, "xl")], axis=0)
    beside = swap(ids, "core")
    ids = jnp.where(core == 0, jnp.stack([ids, beside]), jnp.stack([beside, ids]))
    below = [ids]
    for hop in range(1, 8):
        below.append(lax.ppermute(ids, "z", [(i, (i + hop) % 8) for i in range(8)]))
    ids = jnp.stack(below[::-1] * 2)
    ids = lax.dynamic_slice_in_dim(ids, 7 - z, 8).astype(jnp.int32)

    mine = lax.dynamic_index_in_dim(ids[:, :, 0], core, axis=1, keepdims=False).swapaxes(0, 1)
    near = ((mine >> 10) & 3) ^ quarter
    pool_keys = jnp.where((mine >> 12) == z, (near << 10) | (mine & 1023), -1)
    pool_counts = count_lookups(pool_keys, 4 * BLOCK)
    across_core = swap(columns, "core")
    across_xl = swap(columns, "xl")
    across_both = swap(across_xl, "core")
    partial = pool((columns, across_core, across_xl, across_both), pool_counts)
    pooled = lax.psum_scatter(partial, "z", scatter_dimension=0, tiled=True)[0]
    pooled = pooled.T.astype(jnp.bfloat16)[:, None, :]

    pieces = lax.all_to_all(columns.T.reshape(32, PIECE, -1), ROW, 0, 0, tiled=True)
    lookups = ids.transpose(3, 0, 1, 2, 4).reshape(32, 32, 128)
    place = ((lookups >> 10) + shift[0]) & 31
    keys = jnp.where(((lookups >> 5) & 31) == 4 * z + quarter, (place << 5) | (lookups & 31), -1)
    counts = count_lookups(keys, BLOCK)
    fresh = update(shift, counts, grads, pieces)
    updated = lax.all_to_all(fresh, ROW, 0, 0, tiled=True)
    return pooled, updated.reshape(1, BLOCK, -1)


def solution(mesh):
    split = Mesh(mesh.devices.reshape(8, 8, 2, 2), ("grp",) + ROW)
    return jax.shard_map(
        step,
        mesh=split,
        in_specs=(P(None, ROW, "grp"), P(ROW, "grp", None), P(), P(ROW, "grp", None)),
        out_specs=(P(ROW, "grp", None), P("grp", ROW, None)),
        check_vma=False,
    )
```

time: 189 us -> 211 us (1.12)
  blocking collectives: 0 us -> 20.8 us
  matrix products: 10.1 us -> 0 us
  starting transfers between devices: 27.9 us -> 32.8 us
  local copies, waits for them, and re-layouts: 4.63 us -> 8.98 us
  Pallas kernels: 34.2 us -> 38.3 us
    all_to_all x0 -> x1, blocking collectives: none -> 20.8 us  [step(): lax.all_to_all(jnp.swapaxes(tables, 1, 2), 'grp', 0, 0, tiled=True)]
    ppermute x3 -> x13, starting transfers between devices: 2.13 us -> 21.4 us  [the longest x7 17.6 us: step(): below.append(lax.ppermute(ids, 'z', [(i, (i + hop) % 8) for i in range(8)]))]
    all_to_all x4 -> x2, waiting for transfers between devices: 38.8 us -> 54.3 us  [the longest x1 27.4 us: step(): updated = lax.all_to_all(fresh, ROW, 0, 0, tiled=True)]
    all_to_all x4 -> x2, starting transfers between devices: 25.7 us -> 11.3 us  [the longest x1 7.38 us: step(): lax.all_to_all(columns.T.reshape(32, PIECE, -1), ROW, 0, 0, tiled=True)]
    reduce_scatter x1, waiting for transfers between devices: 13.9 us -> 0.03 us  [step(): pooled = lax.psum_scatter(partial, 'z', scatter_dimension=0, tiled=True)[0]]
    dot_general x1 -> x0, matrix products: 10.1 us -> none  [per_device(): gradient = jnp.dot(update_counts, grads, preferred_element_type=jnp.float32)]
    pallas_call x3 -> x4, Pallas kernels: 34.2 us -> 38.3 us  [the longest x2 18.8 us: count_lookups(): pl.pallas_call(count_kernel, grid=(owners // 8, rows // BLOCK), in_specs=...]
    another operation x0 -> x10, local copies, waits for them, and re-layouts: none -> 2.16 us  [the longest x8 2.11 us: step(): ids = jnp.stack(below[::-1] * 2)]
  transfers between devices with their start and end apart: 9 -> 17, of which waited for: 5 -> 8; matrix products, arithmetic and copies ran while one was open for 10% -> 5% of each run, Pallas kernels for 18% -> 18%
where the time goes in v3:
time: 211 us; the launch traced here: 208 us
  waiting for transfers between devices  86.5 us (41%)
  Pallas kernels  38.3 us (18%)
  starting transfers between devices  32.8 us (16%)
  blocking collectives  20.8 us (10%)
  between operations  15.7 us (7%)
  local copies, waits for them, and re-layouts  8.98 us (4%)
  other arithmetic  5.21 us (2%)
    ppermute x6, waiting for transfers between devices, swap(): return lax.ppermute(values, axis, [(0, 1), (1, 0)])  29.1 us
    all_to_all x1, waiting for transfers between devices, step(): updated = lax.all_to_all(fresh, ROW, 0, 0, tiled=True)  27.4 us
    all_to_all x1, waiting for transfers between devices, step(): lax.all_to_all(columns.T.reshape(32, PIECE, -1), ROW, 0, 0, tiled=True)  26.9 us
    all_to_all x1, blocking collectives, step(): lax.all_to_all(jnp.swapaxes(tables, 1, 2), 'grp', 0, 0, tiled=True)  20.8 us
    pallas_call x2, Pallas kernels, count_lookups(): pl.pallas_call(count_kernel, grid=(owners // 8, rows // BLOCK), in_specs=...  18.8 us
    ppermute x7, starting transfers between devices, step(): below.append(lax.ppermute(ids, 'z', [(i, (i + hop) % 8) for i in range(8)]))  17.6 us
    pallas_call x1, Pallas kernels, update(): pl.pallas_call(update_kernel, grid_spec=pltpu.PrefetchScalarGridSpec(num_...  10.1 us
    pallas_call x1, Pallas kernels, pool(): pl.pallas_call(pool_kernel, grid=(owners // 2,), in_specs=[pl.BlockSpec((...  9.35 us
  transfers between devices with their start and end apart: 17, of which 8 were waited for; matrix products, arithmetic and copies ran while one was open for 5% of the time, Pallas kernels for 18%

profile of v3, /device:TPU:4, one launch (start us, length us, event | category | flops | bytes accessed | tf_op | source)
XLA Modules:
  0.0 208.2 jit_solution(9937907734160838209)
XLA Ops:
  8.0 1.3 collective-permute-start.12
  9.3 4.2 %collective-permute-done.12 = bf16[128,512]{1,0:T(8,128)(2,1)S(1)} collective-permute-done((bf16[128,512]{1,0:T(8,128)(2,1)}, bf16[128,512]{1,0:T(8,128)(2,1)S(1)}, u32[]{:S(2)}, u32[]{:S(2)}) %collective-permute-start.12) | collective-permute-done | bytes 131104 | tf_op jit(solution)/shard_map/ppermute | solution.py:132
  13.6 1.6 pad_maximum_fusion
  15.3 20.8 %all_to_all.15 = bf16[8,64,1024]{2,1,0:T(8,128)(2,1)S(1)} all-to-all(bf16[8,64,1024]{2,1,0:T(8,128)(2,1)} %bitcast.46), channel_id=1, replica_groups=mesh['grp'=8,'z'=8,'xl'=2,'core'=2] {'grp'}, dimensions={0} | all-to-all | bytes 2097152 | tf_op jit(solution)/shard_map/all_to_all | solution.py:144
  37.3 21.2 %collective-permute-done.1.t2 = bf16[512,1024]{1,0:T(8,128)(2,1)S(1)} collective-permute-done((bf16[512,1024]{1,0:T(8,128)(2,1)S(1)}, bf16[512,1024]{1,0:T(8,128)(2,1)S(1)}, u32[]{:S(2)}, u32[]{:S(2)}) %collective-permute-start.1) | collective-permute-done | bytes 1048608 | tf_op jit(solution)/shard_map/ppermute | solution.py:132
  60.4 2.5 %collective-permute-done.3 = s16[1,32,128]{2,1,0:T(8,128)(2,1)S(1)} collective-permute-done((s16[1,32,128]{2,1,0:T(8,128)(2,1)S(1)}, s16[1,32,128]{2,1,0:T(8,128)(2,1)S(1)}, u32[]{:S(2)}, u32[]{:S(2)}) %collective-permute-start.3) | collective-permute-done | bytes 8224 | tf_op jit(solution)/shard_map/ppermute | solution.py:132
  64.2 5.9 %collective-permute-start.5 = (s16[2,2,32,128]{3,2,1,0:T(8,128)(2,1)S(1)}, s16[2,2,32,128]{3,2,1,0:T(8,128)(2,1)S(1)}, u32[]{:S(2)}, u32[]{:S(2)}) collective-permute-start(s16[2,2,32,128]{3,2,1,0:T(8,128)(2,1)S(1)} %add_select_fusion), channel_id=1, source_target_pairs={{0,28},{4,0},{8,4},{12,8},{16,12},{20,16},{24,20},{28,24},{1,29},{... | collective-permute-start | bytes 98312 | tf_op jit(solution)/shard_map/ppermute | solution.py:152
  70.1 1.5 collective-permute-start.6
  72.0 5.0 %collective-permute-start.8 = (s16[2,2,32,128]{3,2,1,0:T(8,128)(2,1)S(1)}, s16[2,2,32,128]{3,2,1,0:T(8,128)(2,1)S(1)}, u32[]{:S(2)}, u32[]{:S(2)}) collective-permute-start(s16[2,2,32,128]{3,2,1,0:T(8,128)(2,1)S(1)} %add_select_fusion), channel_id=1, source_target_pairs={{0,16},{4,20},{8,24},{12,28},{16,0},{20,4},{24,8},{28,12},{1,17},{... | collective-permute-start | bytes 98312 | tf_op jit(solution)/shard_map/ppermute | solution.py:152
  77.1 1.5 collective-permute-start.9
  78.7 1.6 collective-permute-start.10
  80.2 1.6 collective-permute-start.11
  82.2 2.8 %collective-permute-done.9 = s16[2,2,32,128]{3,2,1,0:T(8,128)(2,1)S(1)} collective-permute-done((s16[2,2,32,128]{3,2,1,0:T(8,128)(2,1)S(1)}, s16[2,2,32,128]{3,2,1,0:T(8,128)(2,1)S(1)}, u32[]{:S(2)}, u32[]{:S(2)}) %collective-permute-start.9) | collective-permute-done | bytes 32800 | tf_op jit(solution)/shard_map/ppermute | solution.py:152
  85.5 1.7 stack.70
  88.1 8.3 %count.2.w_ref = bf16[8,4096,128]{2,1,0:T(8,128)(2,1)} custom-call(s32[32,8,128]{2,1,0:T(8,128)} %select_bitcast_fusion.1.keys_ref), custom_call_target="tpu_custom_call" | custom-call | tf_op jit(solution)/shard_map/count/pallas_call | solution.py:65
  96.4 9.3 %pool.1 = f32[8,512,128]{2,1,0:T(8,128)} custom-call(bf16[512,1024]{1,0:T(8,128)(2,1)} %bitcast.42, bf16[512,1024]{1,0:T(8,128)(2,1)} %collective-permute-done.t1, bf16[512,1024]{1,0:T(8,128)(2,1)} %copy-done.2, bf16[512,1024]{1,0:T(8,128)(2,1)} %collective-permute-done.2.t3, bf16[8,4096,128]{2,1,0:T(8,128)(2,1)} %count.2.w_ref), custom_call_target="tpu_custom_call" | custom-call | tf_op jit(solution)/shard_map/pool/pallas_call | solution.py:92
  105.7 2.3 %copy.175 = bf16[1024,512]{1,0:T(8,128)(2,1)} copy(bf16[1024,512]{0,1:T(8,128)(2,1)} %bitcast.43) | data formatting | bytes 2097152 | tf_op jit(solution)/shard_map/transpose | solution.py:167
  108.0 7.4 %all-to-all-start.1 = ((bf16[32,32,512]{2,1,0:T(8,128)(2,1)}), bf16[32,32,512]{2,1,0:T(8,128)(2,1)S(1)}, u32[]{:S(2)}, u32[]{:S(2)}) async-start(bf16[32,32,512]{2,1,0:T(8,128)(2,1)} %bitcast.28), calls=%async_computation.2 | async-start | bytes 2097152 | tf_op jit(solution)/shard_map/all_to_all | solution.py:167
  117.0 1.2 copy.174
  118.2 10.6 %count.3.w_ref = bf16[32,1024,128]{2,1,0:T(8,128)(2,1)} custom-call(s32[32,32,128]{2,1,0:T(8,128)} %bitcast.45), custom_call_target="tpu_custom_call" | custom-call | tf_op jit(solution)/shard_map/count/pallas_call | solution.py:65
  128.7 26.9 %all-to-all-done.1.pieces_ref = bf16[32,32,512]{2,1,0:T(8,128)(2,1)S(1)} async-done(((bf16[32,32,512]{2,1,0:T(8,128)(2,1)}), bf16[32,32,512]{2,1,0:T(8,128)(2,1)S(1)}, u32[]{:S(2)}, u32[]{:S(2)}) %all-to-all-start.1) | async-done | bytes 1048608 | tf_op jit(solution)/shard_map/all_to_all | solution.py:167
  156.6 10.1 %update.1 = bf16[32,32,512]{2,1,0:T(8,128)(2,1)} custom-call(s32[1]{0:T(128)} %dynamic_slice.12.shift_ref, bf16[32,1024,128]{2,1,0:T(8,128)(2,1)} %count.3.w_ref, bf16[4096,512]{1,0:T(8,128)(2,1)} %all-gather.2.cloned.1.call-done.grads_ref, bf16[32,32,512]{2,1,0:T(8,128)(2,1)} %copy-done.1), custom_call_target="tpu_custom_call" | custom-call | tf_op jit(solution)/shard_map/update/pallas_call | solution.py:114
  166.6 3.9 %all-to-all-start.2 = ((bf16[32,32,512]{2,1,0:T(8,128)(2,1)}), bf16[32,32,512]{2,1,0:T(8,128)(2,1)S(1)}, u32[]{:S(2)}, u32[]{:S(2)}) async-start(bf16[32,32,512]{2,1,0:T(8,128)(2,1)} %update.1), calls=%async_computation.3 | async-start | bytes 2097152 | tf_op jit(solution)/shard_map/all_to_all | solution.py:173
  172.4 27.4 %all-to-all-done.2 = bf16[32,32,512]{2,1,0:T(8,128)(2,1)S(1)} async-done(((bf16[32,32,512]{2,1,0:T(8,128)(2,1)}), bf16[32,32,512]{2,1,0:T(8,128)(2,1)S(1)}, u32[]{:S(2)}, u32[]{:S(2)}) %all-to-all-start.2) | async-done | bytes 1048608 | tf_op jit(solution)/shard_map/all_to_all | solution.py:173
  (50 shorter events, 11.8 us)
Async XLA Ops:
  8.0 147.6 %all-gather.2.cloned.1.call-start = ((), (), s32[]{:S(2)}) async-start(), calls=%async_computation.5 | async-start | bytes 4456448 | tf_op jit(solution)/shard_map/all_gather | solution.py:142
  8.0 5.5 %collective-permute-start.12 = (bf16[128,512]{1,0:T(8,128)(2,1)}, bf16[128,512]{1,0:T(8,128)(2,1)S(1)}, u32[]{:S(2)}, u32[]{:S(2)}) collective-permute-start(bf16[128,512]{1,0:T(8,128)(2,1)} %bitcast.47), channel_id=1, source_target_pairs={{0,2},{2,0},{1,3},{3,1},{4,6},{6,4},{5,7},{7,5},{8,10},{10,8},{9,1... | collective-permute-start | bytes 393224 | tf_op jit(solution)/shard_map/ppermute | solution.py:132
  15.2 155.4 %reduce-scatter.2.cloned.1.call-start = ((), (), s32[]{:S(2)}) async-start(), calls=%async_computation.4 | async-start | bytes 2359296 | tf_op jit(solution)/shard_map/reduce_scatter | solution.py:164
  36.1 60.2 %copy-start = (bf16[8,64,1024]{2,1,0:T(8,128)(2,1)}, bf16[8,64,1024]{2,1,0:T(8,128)(2,1)S(1)}, u32[]{:S(2)}) copy-start(bf16[8,64,1024]{2,1,0:T(8,128)(2,1)S(1)} %all_to_all.15) | copy-start | bytes 3145732
  36.1 22.4 %collective-permute-start.1 = (bf16[512,1024]{1,0:T(8,128)(2,1)S(1)}, bf16[512,1024]{1,0:T(8,128)(2,1)S(1)}, u32[]{:S(2)}, u32[]{:S(2)}) collective-permute-start(bf16[512,1024]{1,0:T(8,128)(2,1)S(1)} %bitcast.40), channel_id=1, source_target_pairs={{0,2},{2,0},{1,3},{3,1},{4,6},{6,4},{5,7},{7,5},{8,10},{10,8},{9,1... | collective-permute-start | bytes 3145736 | tf_op jit(solution)/shard_map/ppermute | solution.py:132
  37.3 59.0 %collective-permute-start = (bf16[512,1024]{1,0:T(8,128)(2,1)S(1)}, bf16[512,1024]{1,0:T(8,128)(2,1)}, u32[]{:S(2)}, u32[]{:S(2)}) collective-permute-start(bf16[512,1024]{1,0:T(8,128)(2,1)S(1)} %bitcast.41), channel_id=1, source_target_pairs={{0,1},{1,0},{2,3},{3,2},{4,5},{5,4},{6,7},{7,6},{8,9},{9,8},{10,11... | collective-permute-start | bytes 3145736 | tf_op jit(solution)/shard_map/ppermute | solution.py:132
  58.5 37.8 %copy-start.2 = (bf16[512,1024]{1,0:T(8,128)(2,1)}, bf16[512,1024]{1,0:T(8,128)(2,1)S(1)}, u32[]{:S(2)}) copy-start(bf16[512,1024]{1,0:T(8,128)(2,1)S(1)} %collective-permute-done.1.t2) | copy-start | bytes 3145732
  58.5 37.8 %collective-permute-start.2 = (bf16[512,1024]{1,0:T(8,128)(2,1)S(1)}, bf16[512,1024]{1,0:T(8,128)(2,1)}, u32[]{:S(2)}, u32[]{:S(2)}) collective-permute-start(bf16[512,1024]{1,0:T(8,128)(2,1)S(1)} %collective-permute-done.1.t2), channel_id=1, source_target_pairs={{0,1},{1,0},{2,3},{3,2},{4,5},{5,4},{6,7},{7,6},{8,9},{9,8},{10,11... | collective-permute-start | bytes 3145736 | tf_op jit(solution)/shard_map/ppermute | solution.py:132
  59.2 3.7 %collective-permute-start.3 = (s16[1,32,128]{2,1,0:T(8,128)(2,1)S(1)}, s16[1,32,128]{2,1,0:T(8,128)(2,1)S(1)}, u32[]{:S(2)}, u32[]{:S(2)}) collective-permute-start(s16[1,32,128]{2,1,0:T(8,128)(2,1)S(1)} %convert_bitcast_fusion.1), channel_id=1, source_target_pairs={{0,2},{2,0},{1,3},{3,1},{4,6},{6,4},{5,7},{7,5},{8,10},{10,8},{9,1... | collective-permute-start | bytes 24584 | tf_op jit(solution)/shard_map/ppermute | solution.py:132
  62.9 1.3 collective-permute-start.4
  64.2 7.8 %collective-permute-start.5 = (s16[2,2,32,128]{3,2,1,0:T(8,128)(2,1)S(1)}, s16[2,2,32,128]{3,2,1,0:T(8,128)(2,1)S(1)}, u32[]{:S(2)}, u32[]{:S(2)}) collective-permute-start(s16[2,2,32,128]{3,2,1,0:T(8,128)(2,1)S(1)} %add_select_fusion), channel_id=1, source_target_pairs={{0,28},{4,0},{8,4},{12,8},{16,12},{20,16},{24,20},{28,24},{1,29},{... | collective-permute-start | bytes 98312 | tf_op jit(solution)/shard_map/ppermute | solution.py:152
  70.1 7.0 %collective-permute-start.6 = (s16[2,2,32,128]{3,2,1,0:T(8,128)(2,1)S(1)}, s16[2,2,32,128]{3,2,1,0:T(8,128)(2,1)S(1)}, u32[]{:S(2)}, u32[]{:S(2)}) collective-permute-start(s16[2,2,32,128]{3,2,1,0:T(8,128)(2,1)S(1)} %add_select_fusion), channel_id=1, source_target_pairs={{0,24},{4,28},{8,0},{12,4},{16,8},{20,12},{24,16},{28,20},{1,25},{... | collective-permute-start | bytes 98312 | tf_op jit(solution)/shard_map/ppermute | solution.py:152
  71.6 7.1 %collective-permute-start.7 = (s16[2,2,32,128]{3,2,1,0:T(8,128)(2,1)S(1)}, s16[2,2,32,128]{3,2,1,0:T(8,128)(2,1)S(1)}, u32[]{:S(2)}, u32[]{:S(2)}) collective-permute-start(s16[2,2,32,128]{3,2,1,0:T(8,128)(2,1)S(1)} %add_select_fusion), channel_id=1, source_target_pairs={{0,20},{4,24},{8,28},{12,0},{16,4},{20,8},{24,12},{28,16},{1,21},{... | collective-permute-start | bytes 98312 | tf_op jit(solution)/shard_map/ppermute | solution.py:152
  72.0 8.2 %collective-permute-start.8 = (s16[2,2,32,128]{3,2,1,0:T(8,128)(2,1)S(1)}, s16[2,2,32,128]{3,2,1,0:T(8,128)(2,1)S(1)}, u32[]{:S(2)}, u32[]{:S(2)}) collective-permute-start(s16[2,2,32,128]{3,2,1,0:T(8,128)(2,1)S(1)} %add_select_fusion), channel_id=1, source_target_pairs={{0,16},{4,20},{8,24},{12,28},{16,0},{20,4},{24,8},{28,12},{1,17},{... | collective-permute-start | bytes 98312 | tf_op jit(solution)/shard_map/ppermute | solution.py:152
  77.1 7.9 %collective-permute-start.9 = (s16[2,2,32,128]{3,2,1,0:T(8,128)(2,1)S(1)}, s16[2,2,32,128]{3,2,1,0:T(8,128)(2,1)S(1)}, u32[]{:S(2)}, u32[]{:S(2)}) collective-permute-start(s16[2,2,32,128]{3,2,1,0:T(8,128)(2,1)S(1)} %add_select_fusion), channel_id=1, source_target_pairs={{0,12},{4,16},{8,20},{12,24},{16,28},{20,0},{24,4},{28,8},{1,13},{... | collective-permute-start | bytes 98312 | tf_op jit(solution)/shard_map/ppermute | solution.py:152
  78.7 6.5 %collective-permute-start.10 = (s16[2,2,32,128]{3,2,1,0:T(8,128)(2,1)S(1)}, s16[2,2,32,128]{3,2,1,0:T(8,128)(2,1)S(1)}, u32[]{:S(2)}, u32[]{:S(2)}) collective-permute-start(s16[2,2,32,128]{3,2,1,0:T(8,128)(2,1)S(1)} %add_select_fusion), channel_id=1, source_target_pairs={{0,8},{4,12},{8,16},{12,20},{16,24},{20,28},{24,0},{28,4},{1,9},{5... | collective-permute-start | bytes 98312 | tf_op jit(solution)/shard_map/ppermute | solution.py:152
  80.2 5.2 %collective-permute-start.11 = (s16[2,2,32,128]{3,2,1,0:T(8,128)(2,1)S(1)}, s16[2,2,32,128]{3,2,1,0:T(8,128)(2,1)S(1)}, u32[]{:S(2)}, u32[]{:S(2)}) collective-permute-start(s16[2,2,32,128]{3,2,1,0:T(8,128)(2,1)S(1)} %add_select_fusion), channel_id=1, source_target_pairs={{0,4},{4,8},{8,12},{12,16},{16,20},{20,24},{24,28},{28,0},{1,5},{5... | collective-permute-start | bytes 98312 | tf_op jit(solution)/shard_map/ppermute | solution.py:152
  96.3 19.1 %copy-start.3 = (s32[8]{0:T(128)S(1)}, s32[8]{0:T(128)}, u32[]{:S(2)}) copy-start(s32[8]{0:T(128)} %param.6) | copy-start | bytes 100
  108.0 47.6 %all-to-all-start.1 = ((bf16[32,32,512]{2,1,0:T(8,128)(2,1)}), bf16[32,32,512]{2,1,0:T(8,128)(2,1)S(1)}, u32[]{:S(2)}, u32[]{:S(2)}) async-start(bf16[32,32,512]{2,1,0:T(8,128)(2,1)} %bitcast.28), calls=%async_computation.2 | async-start | bytes 2097152 | tf_op jit(solution)/shard_map/all_to_all | solution.py:167
  155.6 1.0 copy-start.1
  166.6 33.1 %all-to-all-start.2 = ((bf16[32,32,512]{2,1,0:T(8,128)(2,1)}), bf16[32,32,512]{2,1,0:T(8,128)(2,1)S(1)}, u32[]{:S(2)}, u32[]{:S(2)}) async-start(bf16[32,32,512]{2,1,0:T(8,128)(2,1)} %update.1), calls=%async_computation.3 | async-start | bytes 2097152 | tf_op jit(solution)/shard_map/all_to_all | solution.py:173
Sparse Core Ops, SparseCore 0:
  15.3 44.9 all-gather.1
Sparse Core Ops, SparseCore 1:
  105.8 59.7 reduce-scatter.1

commit v4 on v3

--- a/solution.py
+++ b/solution.py
@@ -92,7 +92,7 @@
     return pl.pallas_call(
         pool_kernel,
         grid=(owners // 2,),
-        in_specs=[pl.BlockSpec((dim, BLOCK), lambda n: (0, 0))] * 4
+        in_specs=[pl.BlockSpec(memory_space=pltpu.VMEM)] * 4
         + [pl.BlockSpec((2, rows, lanes), lambda n: (n, 0, 0))],
         out_specs=pl.BlockSpec((2, dim, lanes), lambda n: (n, 0, 0)),
         out_shape=jax.ShapeDtypeStruct((owners, dim, lanes), jnp.float32),
@@ -100,32 +100,46 @@
     )(*tables, counts)
 
 
-def update_kernel(shift_ref, w_ref, grads_ref, pieces_ref, out_ref):
-    step = pl.program_id(0)
-    gradient = jnp.dot(side_by_side(w_ref), grads_ref[...], preferred_element_type=jnp.float32)
-    for i in range(out_ref.shape[0]):
-        old = pieces_ref[(8 * step + i - shift_ref[0]) & 31].astype(jnp.float32)
-        out_ref[i] = (old - STEP_RATE * gradient[i * PIECE : (i + 1) * PIECE]).astype(jnp.bfloat16)
+def gradient_kernel(w_ref, grads_ref, out_ref):
+    out_ref[...] = jnp.dot(side_by_side(w_ref), grads_ref[...], preferred_element_type=jnp.float32)
 
 
-def update(shift, counts, grads, pieces):
+def row_gradient(counts, grads):
     owners, rows, lanes = counts.shape
-    samples, dim = grads.shape
+    dim = grads.shape[1]
+    return pl.pallas_call(
+        gradient_kernel,
+        grid=(rows // 256,),
+        in_specs=[pl.BlockSpec((owners, 256, lanes), lambda n: (0, n, 0)), pl.BlockSpec(grads.shape, lambda n: (0, 0))],
+        out_specs=pl.BlockSpec((256, dim), lambda n: (n, 0)),
+        out_shape=jax.ShapeDtypeStruct((rows, dim), jnp.float32),
+        name="gradient",
+    )(counts, grads)
+
+
+def update_kernel(shift_ref, gradient_ref, pieces_ref, out_ref):
+    for i in range(out_ref.shape[0]):
+        step = STEP_RATE * gradient_ref[i * PIECE : (i + 1) * PIECE]
+        old = pieces_ref[(8 * pl.program_id(0) + i - shift_ref[0]) & 31].astype(jnp.float32)
+        out_ref[i] = (old - step).astype(jnp.bfloat16)
+
+
+def update(shift, gradient, pieces):
+    dim = gradient.shape[1]
     return pl.pallas_call(
         update_kernel,
         grid_spec=pltpu.PrefetchScalarGridSpec(
             num_scalar_prefetch=1,
-            grid=(rows // 256,),
+            grid=(4,),
             in_specs=[
-                pl.BlockSpec((owners, 256, lanes), lambda n, s: (0, n, 0)),
-                pl.BlockSpec((samples, dim), lambda n, s: (0, 0)),
-                pl.BlockSpec(pieces.shape, lambda n, s: (0, 0, 0)),
+                pl.BlockSpec((8 * PIECE, dim), lambda n, s: (n, 0)),
+                pl.BlockSpec(memory_space=pltpu.VMEM),
             ],
             out_specs=pl.BlockSpec((8, PIECE, dim), lambda n, s: (n, 0, 0)),
         ),
         out_shape=jax.ShapeDtypeStruct(pieces.shape, jnp.bfloat16),
         name="update",
-    )(shift, counts, grads, pieces)
+    )(shift, gradient, pieces)
 
 
 def swap(values, axis):
@@ -143,19 +157,12 @@
 
     columns = lax.all_to_all(jnp.swapaxes(tables, 1, 2), "grp", 0, 0, tiled=True).reshape(-1, BLOCK)
 
-    ids = indices[:, 0, :].T.astype(jnp.int16)[None]
-    ids = jnp.concatenate([ids, swap(ids, "xl")], axis=0)
-    beside = swap(ids, "core")
-    ids = jnp.where(core == 0, jnp.stack([ids, beside]), jnp.stack([beside, ids]))
-    below = [ids]
-    for hop in range(1, 8):
-        below.append(lax.ppermute(ids, "z", [(i, (i + hop) % 8) for i in range(8)]))
-    ids = jnp.stack(below[::-1] * 2)
-    ids = lax.dynamic_slice_in_dim(ids, 7 - z, 8).astype(jnp.int32)
+    mine = indices[:, 0, :].T.astype(jnp.int16)
+    mine = lax.all_to_all(jnp.broadcast_to(mine, (8,) + mine.shape), "z", 0, 0, tiled=True)
 
-    mine = lax.dynamic_index_in_dim(ids[:, :, 0], core, axis=1, keepdims=False).swapaxes(0, 1)
-    near = ((mine >> 10) & 3) ^ quarter
-    pool_keys = jnp.where((mine >> 12) == z, (near << 10) | (mine & 1023), -1)
+    lookups = mine.astype(jnp.int32).swapaxes(0, 1)
+    near = ((lookups >> 10) & 3) ^ quarter
+    pool_keys = jnp.where((lookups >> 12) == z, (near << 10) | (lookups & 1023), -1)
     pool_counts = count_lookups(pool_keys, 4 * BLOCK)
     across_core = swap(columns, "core")
     across_xl = swap(columns, "xl")
@@ -165,11 +172,15 @@
     pooled = pooled.T.astype(jnp.bfloat16)[:, None, :]
 
     pieces = lax.all_to_all(columns.T.reshape(32, PIECE, -1), ROW, 0, 0, tiled=True)
-    lookups = ids.transpose(3, 0, 1, 2, 4).reshape(32, 32, 128)
+    both = jnp.stack([mine, swap(mine, "xl")], axis=1)
+    beside = swap(both, "core")
+    lookups = jnp.where(core == 0, jnp.stack([both, beside], axis=1), jnp.stack([beside, both], axis=1))
+    lookups = lookups.astype(jnp.int32).transpose(3, 0, 1, 2, 4).reshape(32, 32, 128)
     place = ((lookups >> 10) + shift[0]) & 31
     keys = jnp.where(((lookups >> 5) & 31) == 4 * z + quarter, (place << 5) | (lookups & 31), -1)
     counts = count_lookups(keys, BLOCK)
-    fresh = update(shift, counts, grads, pieces)
+    gradient = row_gradient(counts, grads)
+    fresh = update(shift, gradient, pieces)
     updated = lax.all_to_all(fresh, ROW, 0, 0, tiled=True)
     return pooled, updated.reshape(1, BLOCK, -1)
 

time: 211 us -> 194 us (0.919)
  the two profiles are of different devices: /device:TPU:4 before, /device:TPU:3 now
where the time goes in v4:
time: 194 us; the launch traced here: 193 us
  waiting for transfers between devices  71.1 us (37%)
  Pallas kernels  42.5 us (22%)
  starting transfers between devices  30.7 us (16%)
  blocking collectives  20.5 us (11%)
  between operations  15.6 us (8%)
  local copies, waits for them, and re-layouts  7.43 us (4%)
  other arithmetic  4.95 us (3%)
    all_to_all x1, waiting for transfers between devices, step(): updated = lax.all_to_all(fresh, ROW, 0, 0, tiled=True)  27.2 us
    ppermute x6, waiting for transfers between devices, swap(): return lax.ppermute(values, axis, [(0, 1), (1, 0)])  25 us
    all_to_all x1, blocking collectives, step(): lax.all_to_all(jnp.swapaxes(tables, 1, 2), 'grp', 0, 0, tiled=True)  20.5 us
    pallas_call x2, Pallas kernels, count_lookups(): pl.pallas_call(count_kernel, grid=(owners // 8, rows // BLOCK), in_specs=...  18.8 us
    all_to_all x1, waiting for transfers between devices, step(): lax.all_to_all(columns.T.reshape(32, PIECE, -1), ROW, 0, 0, tiled=True)  11.9 us
    ppermute x6, starting transfers between devices, swap(): return lax.ppermute(values, axis, [(0, 1), (1, 0)])  10.5 us
    pallas_call x1, Pallas kernels, pool(): pl.pallas_call(pool_kernel, grid=(owners // 2,), in_specs=[pl.BlockSpec(m...  9.74 us
    pallas_call x1, Pallas kernels, row_gradient(): pl.pallas_call(gradient_kernel, grid=(rows // 256,), in_specs=[pl.BlockSp...  9.33 us
  transfers between devices with their start and end apart: 11, of which 7 were waited for; matrix products, arithmetic and copies ran while one was open for 4% of the time, Pallas kernels for 22%

profile of v4, /device:TPU:3, one launch (start us, length us, event | category | flops | bytes accessed | tf_op | source)
XLA Modules:
  0.0 192.8 jit_solution(4340001122319251726)
XLA Ops:
  8.1 4.4 %collective-permute-done.5 = bf16[128,512]{1,0:T(8,128)(2,1)S(1)} collective-permute-done((bf16[128,512]{1,0:T(8,128)(2,1)}, bf16[128,512]{1,0:T(8,128)(2,1)S(1)}, u32[]{:S(2)}, u32[]{:S(2)}) %collective-permute-start.5) | collective-permute-done | bytes 131104 | tf_op jit(solution)/shard_map/ppermute | solution.py:146
  12.5 1.6 pad_maximum_fusion
  14.1 20.5 %all_to_all.20 = bf16[8,64,1024]{2,1,0:T(8,128)(2,1)S(1)} all-to-all(bf16[8,64,1024]{2,1,0:T(8,128)(2,1)} %bitcast.34), channel_id=1, replica_groups=mesh['grp'=8,'z'=8,'xl'=2,'core'=2] {'grp'}, dimensions={0} | all-to-all | bytes 2097152 | tf_op jit(solution)/shard_map/all_to_all | solution.py:158
  34.6 1.2 collective-permute-start.1
  35.8 3.9 %collective-permute-start = (bf16[512,1024]{1,0:T(8,128)(2,1)S(1)}, bf16[512,1024]{1,0:T(8,128)(2,1)S(1)}, u32[]{:S(2)}, u32[]{:S(2)}) collective-permute-start(bf16[512,1024]{1,0:T(8,128)(2,1)S(1)} %bitcast.29), channel_id=1, source_target_pairs={{0,1},{1,0},{2,3},{3,2},{4,5},{5,4},{6,7},{7,6},{8,9},{9,8},{10,11... | collective-permute-start | bytes 3145736 | tf_op jit(solution)/shard_map/ppermute | solution.py:146
  39.7 16.2 %collective-permute-done.1.t2 = bf16[512,1024]{1,0:T(8,128)(2,1)S(1)} collective-permute-done((bf16[512,1024]{1,0:T(8,128)(2,1)S(1)}, bf16[512,1024]{1,0:T(8,128)(2,1)S(1)}, u32[]{:S(2)}, u32[]{:S(2)}) %collective-permute-start.1) | collective-permute-done | bytes 1048608 | tf_op jit(solution)/shard_map/ppermute | solution.py:146
  55.8 4.4 %collective-permute-start.2 = (bf16[512,1024]{1,0:T(8,128)(2,1)S(1)}, bf16[512,1024]{1,0:T(8,128)(2,1)}, u32[]{:S(2)}, u32[]{:S(2)}) collective-permute-start(bf16[512,1024]{1,0:T(8,128)(2,1)S(1)} %collective-permute-done.1.t2), channel_id=1, source_target_pairs={{0,1},{1,0},{2,3},{3,2},{4,5},{5,4},{6,7},{7,6},{8,9},{9,8},{10,11... | collective-permute-start | bytes 3145736 | tf_op jit(solution)/shard_map/ppermute | solution.py:146
  61.6 8.2 %all-to-all-start.1 = ((s16[8,32,128]{2,1,0:T(8,128)(2,1)}), s16[8,32,128]{2,1,0:T(8,128)(2,1)S(1)}, u32[]{:S(2)}, u32[]{:S(2)}) async-start(s16[8,32,128]{2,1,0:T(8,128)(2,1)} %broadcast_in_dim.14), calls=%async_computation.1 | async-start | bytes 131072 | tf_op jit(solution)/shard_map/all_to_all | solution.py:161
  69.8 7.1 %all-to-all-done.1 = s16[8,32,128]{2,1,0:T(8,128)(2,1)S(1)} async-done(((s16[8,32,128]{2,1,0:T(8,128)(2,1)}), s16[8,32,128]{2,1,0:T(8,128)(2,1)S(1)}, u32[]{:S(2)}, u32[]{:S(2)}) %all-to-all-start.1) | async-done | bytes 65568 | tf_op jit(solution)/shard_map/all_to_all | solution.py:161
  77.6 8.3 %count.2.w_ref = bf16[8,4096,128]{2,1,0:T(8,128)(2,1)} custom-call(s32[32,8,128]{2,1,0:T(8,128)} %fusion.14.keys_ref), custom_call_target="tpu_custom_call" | custom-call | tf_op jit(solution)/shard_map/count/pallas_call | solution.py:65
  86.9 9.7 %pool.1 = f32[8,512,128]{2,1,0:T(8,128)} custom-call(bf16[512,1024]{1,0:T(8,128)(2,1)} %bitcast.30, bf16[512,1024]{1,0:T(8,128)(2,1)} %copy-done.4, bf16[512,1024]{1,0:T(8,128)(2,1)} %copy-done.3, bf16[512,1024]{1,0:T(8,128)(2,1)} %collective-permute-done.2.t3, bf16[8,4096,128]{2,1,0:T(8,128)(2,1)} %count.2.w_ref), custom_call_target="tpu_custom_call" | custom-call | tf_op jit(solution)/shard_map/pool/pallas_call | solution.py:92
  96.7 1.3 copy.11
  98.0 7.1 %all-to-all-start.2 = ((bf16[32,32,512]{2,1,0:T(8,128)(2,1)}), bf16[32,32,512]{2,1,0:T(8,128)(2,1)S(1)}, u32[]{:S(2)}, u32[]{:S(2)}) async-start(bf16[32,32,512]{2,1,0:T(8,128)(2,1)} %bitcast.17), calls=%async_computation.3 | async-start | bytes 2097152 | tf_op jit(solution)/shard_map/all_to_all | solution.py:174
  105.3 4.0 %collective-permute-done.3 = s16[8,32,128]{2,1,0:T(8,128)(2,1)S(1)} collective-permute-done((s16[8,32,128]{2,1,0:T(8,128)(2,1)S(1)}, s16[8,32,128]{2,1,0:T(8,128)(2,1)S(1)}, u32[]{:S(2)}, u32[]{:S(2)}) %collective-permute-start.3) | collective-permute-done | bytes 65568 | tf_op jit(solution)/shard_map/ppermute | solution.py:146
  112.1 1.2 copy.10
  113.3 10.5 %count.3.w_ref = bf16[32,1024,128]{2,1,0:T(8,128)(2,1)} custom-call(s32[32,32,128]{2,1,0:T(8,128)} %bitcast.33), custom_call_target="tpu_custom_call" | custom-call | tf_op jit(solution)/shard_map/count/pallas_call | solution.py:65
  123.9 9.3 %gradient.1.gradient_ref = f32[1024,512]{1,0:T(8,128)} custom-call(bf16[32,1024,128]{2,1,0:T(8,128)(2,1)} %count.3.w_ref, bf16[4096,512]{1,0:T(8,128)(2,1)} %all-gather.2.cloned.1.call-done.grads_ref), custom_call_target="tpu_custom_call" | custom-call | tf_op jit(solution)/shard_map/gradient/pallas_call | solution.py:110
  133.2 11.9 %all-to-all-done.2.pieces_ref = bf16[32,32,512]{2,1,0:T(8,128)(2,1)S(1)} async-done(((bf16[32,32,512]{2,1,0:T(8,128)(2,1)}), bf16[32,32,512]{2,1,0:T(8,128)(2,1)S(1)}, u32[]{:S(2)}, u32[]{:S(2)}) %all-to-all-start.2) | async-done | bytes 1048608 | tf_op jit(solution)/shard_map/all_to_all | solution.py:174
  145.1 1.0 copy-done.2
  146.0 4.7 %update.1 = bf16[32,32,512]{2,1,0:T(8,128)(2,1)} custom-call(s32[1]{0:T(128)} %dynamic_slice.3.shift_ref, f32[1024,512]{1,0:T(8,128)} %gradient.1.gradient_ref, bf16[32,32,512]{2,1,0:T(8,128)(2,1)} %copy-done.2), custom_call_target="tpu_custom_call" | custom-call | tf_op jit(solution)/shard_map/update/pallas_call | solution.py:129
  150.7 4.7 %all-to-all-start.3 = ((bf16[32,32,512]{2,1,0:T(8,128)(2,1)}), bf16[32,32,512]{2,1,0:T(8,128)(2,1)S(1)}, u32[]{:S(2)}, u32[]{:S(2)}) async-start(bf16[32,32,512]{2,1,0:T(8,128)(2,1)} %update.1), calls=%async_computation.4 | async-start | bytes 2097152 | tf_op jit(solution)/shard_map/all_to_all | solution.py:184
  155.5 1.0 convert_bitcast_fusion
  157.2 27.2 %all-to-all-done.3 = bf16[32,32,512]{2,1,0:T(8,128)(2,1)S(1)} async-done(((bf16[32,32,512]{2,1,0:T(8,128)(2,1)}), bf16[32,32,512]{2,1,0:T(8,128)(2,1)S(1)}, u32[]{:S(2)}, u32[]{:S(2)}) %all-to-all-start.3) | async-done | bytes 1048608 | tf_op jit(solution)/shard_map/all_to_all | solution.py:184
  184.4 1.0 copy.15
  (30 shorter events, 7.0 us)
Async XLA Ops:
  8.0 115.9 %all-gather.2.cloned.1.call-start = ((), (), s32[]{:S(2)}) async-start(), calls=%async_computation.6 | async-start | bytes 4456448 | tf_op jit(solution)/shard_map/all_gather | solution.py:156
  8.0 4.5 %collective-permute-start.5 = (bf16[128,512]{1,0:T(8,128)(2,1)}, bf16[128,512]{1,0:T(8,128)(2,1)S(1)}, u32[]{:S(2)}, u32[]{:S(2)}) collective-permute-start(bf16[128,512]{1,0:T(8,128)(2,1)} %bitcast.36), channel_id=1, source_target_pairs={{0,2},{2,0},{1,3},{3,1},{4,6},{6,4},{5,7},{7,5},{8,10},{10,8},{9,1... | collective-permute-start | bytes 393224 | tf_op jit(solution)/shard_map/ppermute | solution.py:146
  34.6 51.3 %copy-start = (bf16[8,64,1024]{2,1,0:T(8,128)(2,1)}, bf16[8,64,1024]{2,1,0:T(8,128)(2,1)S(1)}, u32[]{:S(2)}) copy-start(bf16[8,64,1024]{2,1,0:T(8,128)(2,1)S(1)} %all_to_all.20) | copy-start | bytes 3145732
  34.6 21.2 %collective-permute-start.1 = (bf16[512,1024]{1,0:T(8,128)(2,1)S(1)}, bf16[512,1024]{1,0:T(8,128)(2,1)S(1)}, u32[]{:S(2)}, u32[]{:S(2)}) collective-permute-start(bf16[512,1024]{1,0:T(8,128)(2,1)S(1)} %bitcast.28), channel_id=1, source_target_pairs={{0,2},{2,0},{1,3},{3,1},{4,6},{6,4},{5,7},{7,5},{8,10},{10,8},{9,1... | collective-permute-start | bytes 3145736 | tf_op jit(solution)/shard_map/ppermute | solution.py:146
  35.8 50.1 %collective-permute-start = (bf16[512,1024]{1,0:T(8,128)(2,1)S(1)}, bf16[512,1024]{1,0:T(8,128)(2,1)S(1)}, u32[]{:S(2)}, u32[]{:S(2)}) collective-permute-start(bf16[512,1024]{1,0:T(8,128)(2,1)S(1)} %bitcast.29), channel_id=1, source_target_pairs={{0,1},{1,0},{2,3},{3,2},{4,5},{5,4},{6,7},{7,6},{8,9},{9,8},{10,11... | collective-permute-start | bytes 3145736 | tf_op jit(solution)/shard_map/ppermute | solution.py:146
  55.8 30.1 %copy-start.3 = (bf16[512,1024]{1,0:T(8,128)(2,1)}, bf16[512,1024]{1,0:T(8,128)(2,1)S(1)}, u32[]{:S(2)}) copy-start(bf16[512,1024]{1,0:T(8,128)(2,1)S(1)} %collective-permute-done.1.t2) | copy-start | bytes 3145732
  55.8 30.1 %collective-permute-start.2 = (bf16[512,1024]{1,0:T(8,128)(2,1)S(1)}, bf16[512,1024]{1,0:T(8,128)(2,1)}, u32[]{:S(2)}, u32[]{:S(2)}) collective-permute-start(bf16[512,1024]{1,0:T(8,128)(2,1)S(1)} %collective-permute-done.1.t2), channel_id=1, source_target_pairs={{0,1},{1,0},{2,3},{3,2},{4,5},{5,4},{6,7},{7,6},{8,9},{9,8},{10,11... | collective-permute-start | bytes 3145736 | tf_op jit(solution)/shard_map/ppermute | solution.py:146
  61.6 15.3 %all-to-all-start.1 = ((s16[8,32,128]{2,1,0:T(8,128)(2,1)}), s16[8,32,128]{2,1,0:T(8,128)(2,1)S(1)}, u32[]{:S(2)}, u32[]{:S(2)}) async-start(s16[8,32,128]{2,1,0:T(8,128)(2,1)} %broadcast_in_dim.14), calls=%async_computation.1 | async-start | bytes 131072 | tf_op jit(solution)/shard_map/all_to_all | solution.py:161
  69.8 85.7 %reduce-scatter.2.cloned.1.call-start = ((), (), s32[]{:S(2)}) async-start(), calls=%async_computation.5 | async-start | bytes 2359296 | tf_op jit(solution)/shard_map/reduce_scatter | solution.py:171
  85.9 1.0 copy-start.4
  85.9 10.7 %copy-start.1 = (bf16[8,64,1024]{2,1,0:T(8,128)(2,1)S(1)}, bf16[8,64,1024]{2,1,0:T(8,128)(2,1)}, u32[]{:S(2)}) copy-start(bf16[8,64,1024]{2,1,0:T(8,128)(2,1)} %copy-done) | copy-start | bytes 3145732
  96.6 13.6 %copy-start.5 = (s32[8]{0:T(128)S(1)}, s32[8]{0:T(128)}, u32[]{:S(2)}) copy-start(s32[8]{0:T(128)} %param.6) | copy-start | bytes 100
  98.0 47.1 %all-to-all-start.2 = ((bf16[32,32,512]{2,1,0:T(8,128)(2,1)}), bf16[32,32,512]{2,1,0:T(8,128)(2,1)S(1)}, u32[]{:S(2)}, u32[]{:S(2)}) async-start(bf16[32,32,512]{2,1,0:T(8,128)(2,1)} %bitcast.17), calls=%async_computation.3 | async-start | bytes 2097152 | tf_op jit(solution)/shard_map/all_to_all | solution.py:174
  105.1 4.2 %collective-permute-start.3 = (s16[8,32,128]{2,1,0:T(8,128)(2,1)S(1)}, s16[8,32,128]{2,1,0:T(8,128)(2,1)S(1)}, u32[]{:S(2)}, u32[]{:S(2)}) collective-permute-start(s16[8,32,128]{2,1,0:T(8,128)(2,1)S(1)} %all-to-all-done.1), channel_id=1, source_target_pairs={{0,2},{2,0},{1,3},{3,1},{4,6},{6,4},{5,7},{7,5},{8,10},{10,8},{9,1... | collective-permute-start | bytes 196616 | tf_op jit(solution)/shard_map/ppermute | solution.py:146
  109.4 1.9 collective-permute-start.4
  145.1 1.0 copy-start.2
  150.7 33.7 %all-to-all-start.3 = ((bf16[32,32,512]{2,1,0:T(8,128)(2,1)}), bf16[32,32,512]{2,1,0:T(8,128)(2,1)S(1)}, u32[]{:S(2)}, u32[]{:S(2)}) async-start(bf16[32,32,512]{2,1,0:T(8,128)(2,1)} %update.1), calls=%async_computation.4 | async-start | bytes 2097152 | tf_op jit(solution)/shard_map/all_to_all | solution.py:184
Sparse Core Ops, SparseCore 0:
  14.3 46.4 all-gather.1
Sparse Core Ops, SparseCore 1:
  96.7 54.0 reduce-scatter.1

commit v5 on v3

--- a/solution.py
+++ b/solution.py
@@ -92,7 +92,7 @@
     return pl.pallas_call(
         pool_kernel,
         grid=(owners // 2,),
-        in_specs=[pl.BlockSpec((dim, BLOCK), lambda n: (0, 0))] * 4
+        in_specs=[pl.BlockSpec(memory_space=pltpu.VMEM)] * 4
         + [pl.BlockSpec((2, rows, lanes), lambda n: (n, 0, 0))],
         out_specs=pl.BlockSpec((2, dim, lanes), lambda n: (n, 0, 0)),
         out_shape=jax.ShapeDtypeStruct((owners, dim, lanes), jnp.float32),
@@ -101,10 +101,9 @@
 
 
 def update_kernel(shift_ref, w_ref, grads_ref, pieces_ref, out_ref):
-    step = pl.program_id(0)
     gradient = jnp.dot(side_by_side(w_ref), grads_ref[...], preferred_element_type=jnp.float32)
     for i in range(out_ref.shape[0]):
-        old = pieces_ref[(8 * step + i - shift_ref[0]) & 31].astype(jnp.float32)
+        old = pieces_ref[(8 * pl.program_id(0) + i - shift_ref[0]) & 31].astype(jnp.float32)
         out_ref[i] = (old - STEP_RATE * gradient[i * PIECE : (i + 1) * PIECE]).astype(jnp.bfloat16)
 
 
@@ -138,24 +137,18 @@
     shift = lax.dynamic_slice_in_dim(block_shift, lax.axis_index("grp"), 1)
 
     own = pooled_grad[:, 0, :]
-    own = jnp.concatenate([own, swap(own, "xl")], axis=0)
+    across = swap(own, "xl")
+    own = jnp.concatenate([own, across], axis=0)
     grads = lax.all_gather(own, ("z", "core"), axis=0, tiled=True)
 
     columns = lax.all_to_all(jnp.swapaxes(tables, 1, 2), "grp", 0, 0, tiled=True).reshape(-1, BLOCK)
 
-    ids = indices[:, 0, :].T.astype(jnp.int16)[None]
-    ids = jnp.concatenate([ids, swap(ids, "xl")], axis=0)
-    beside = swap(ids, "core")
-    ids = jnp.where(core == 0, jnp.stack([ids, beside]), jnp.stack([beside, ids]))
-    below = [ids]
-    for hop in range(1, 8):
-        below.append(lax.ppermute(ids, "z", [(i, (i + hop) % 8) for i in range(8)]))
-    ids = jnp.stack(below[::-1] * 2)
-    ids = lax.dynamic_slice_in_dim(ids, 7 - z, 8).astype(jnp.int32)
+    mine = indices[:, 0, :].T.astype(jnp.int16)
+    mine = lax.all_to_all(jnp.broadcast_to(mine, (8,) + mine.shape), "z", 0, 0, tiled=True)
 
-    mine = lax.dynamic_index_in_dim(ids[:, :, 0], core, axis=1, keepdims=False).swapaxes(0, 1)
-    near = ((mine >> 10) & 3) ^ quarter
-    pool_keys = jnp.where((mine >> 12) == z, (near << 10) | (mine & 1023), -1)
+    lookups = mine.astype(jnp.int32).swapaxes(0, 1)
+    near = ((lookups >> 10) & 3) ^ quarter
+    pool_keys = jnp.where((lookups >> 12) == z, (near << 10) | (lookups & 1023), -1)
     pool_counts = count_lookups(pool_keys, 4 * BLOCK)
     across_core = swap(columns, "core")
     across_xl = swap(columns, "xl")
@@ -165,7 +158,10 @@
     pooled = pooled.T.astype(jnp.bfloat16)[:, None, :]
 
     pieces = lax.all_to_all(columns.T.reshape(32, PIECE, -1), ROW, 0, 0, tiled=True)
-    lookups = ids.transpose(3, 0, 1, 2, 4).reshape(32, 32, 128)
+    both = jnp.stack([mine, swap(mine, "xl")], axis=1)
+    beside = swap(both, "core")
+    lookups = jnp.where(core == 0, jnp.stack([both, beside], axis=1), jnp.stack([beside, both], axis=1))
+    lookups = lookups.astype(jnp.int32).transpose(3, 0, 1, 2, 4).reshape(32, 32, 128)
     place = ((lookups >> 10) + shift[0]) & 31
     keys = jnp.where(((lookups >> 5) & 31) == 4 * z + quarter, (place << 5) | (lookups & 31), -1)
     counts = count_lookups(keys, BLOCK)

time: 211 us -> 199 us (0.943)
  the two profiles are of different devices: /device:TPU:4 before, /device:TPU:3 now
where the time goes in v5:
time: 199 us
  waiting for transfers between devices  80.9 us (41%)
  Pallas kernels  38.2 us (19%)
  starting transfers between devices  30.2 us (15%)
  blocking collectives  20.5 us (10%)
  between operations  15.6 us (8%)
  local copies, waits for them, and re-layouts  8.39 us (4%)
  other arithmetic  4.95 us (2%)
    all_to_all x1, waiting for transfers between devices, step(): updated = lax.all_to_all(fresh, ROW, 0, 0, tiled=True)  27.2 us
    ppermute x6, waiting for transfers between devices, swap(): return lax.ppermute(values, axis, [(0, 1), (1, 0)])  25 us
    all_to_all x1, waiting for transfers between devices, step(): lax.all_to_all(columns.T.reshape(32, PIECE, -1), ROW, 0, 0, tiled=True)  21.6 us
    all_to_all x1, blocking collectives, step(): lax.all_to_all(jnp.swapaxes(tables, 1, 2), 'grp', 0, 0, tiled=True)  20.5 us
    pallas_call x2, Pallas kernels, count_lookups(): pl.pallas_call(count_kernel, grid=(owners // 8, rows // BLOCK), in_specs=...  18.8 us
    ppermute x6, starting transfers between devices, swap(): return lax.ppermute(values, axis, [(0, 1), (1, 0)])  10.5 us
    pallas_call x1, Pallas kernels, update(): pl.pallas_call(update_kernel, grid_spec=pltpu.PrefetchScalarGridSpec(num_...  10.1 us
    pallas_call x1, Pallas kernels, pool(): pl.pallas_call(pool_kernel, grid=(owners // 2,), in_specs=[pl.BlockSpec(m...  9.34 us
  transfers between devices with their start and end apart: 11, of which 7 were waited for; matrix products, arithmetic and copies ran while one was open for 4% of the time, Pallas kernels for 19%

profile of v5, /device:TPU:3, one launch (start us, length us, event | category | flops | bytes accessed | tf_op | source)
XLA Modules:
  0.0 198.7 jit_solution(3665131675448972792)
XLA Ops:
  8.1 4.4 %collective-permute-done.5 = bf16[128,512]{1,0:T(8,128)(2,1)S(1)} collective-permute-done((bf16[128,512]{1,0:T(8,128)(2,1)}, bf16[128,512]{1,0:T(8,128)(2,1)S(1)}, u32[]{:S(2)}, u32[]{:S(2)}) %collective-permute-start.5) | collective-permute-done | bytes 131104 | tf_op jit(solution)/shard_map/ppermute | solution.py:131
  12.5 1.6 pad_maximum_fusion
  14.1 20.5 %all_to_all.20 = bf16[8,64,1024]{2,1,0:T(8,128)(2,1)S(1)} all-to-all(bf16[8,64,1024]{2,1,0:T(8,128)(2,1)} %bitcast.34), channel_id=1, replica_groups=mesh['grp'=8,'z'=8,'xl'=2,'core'=2] {'grp'}, dimensions={0} | all-to-all | bytes 2097152 | tf_op jit(solution)/shard_map/all_to_all | solution.py:144
  34.6 1.2 collective-permute-start.1
  35.8 3.9 %collective-permute-start = (bf16[512,1024]{1,0:T(8,128)(2,1)S(1)}, bf16[512,1024]{1,0:T(8,128)(2,1)S(1)}, u32[]{:S(2)}, u32[]{:S(2)}) collective-permute-start(bf16[512,1024]{1,0:T(8,128)(2,1)S(1)} %bitcast.29), channel_id=1, source_target_pairs={{0,1},{1,0},{2,3},{3,2},{4,5},{5,4},{6,7},{7,6},{8,9},{9,8},{10,11... | collective-permute-start | bytes 3145736 | tf_op jit(solution)/shard_map/ppermute | solution.py:131
  39.7 16.2 %collective-permute-done.1.t2 = bf16[512,1024]{1,0:T(8,128)(2,1)S(1)} collective-permute-done((bf16[512,1024]{1,0:T(8,128)(2,1)S(1)}, bf16[512,1024]{1,0:T(8,128)(2,1)S(1)}, u32[]{:S(2)}, u32[]{:S(2)}) %collective-permute-start.1) | collective-permute-done | bytes 1048608 | tf_op jit(solution)/shard_map/ppermute | solution.py:131
  55.8 4.4 %collective-permute-start.2 = (bf16[512,1024]{1,0:T(8,128)(2,1)S(1)}, bf16[512,1024]{1,0:T(8,128)(2,1)}, u32[]{:S(2)}, u32[]{:S(2)}) collective-permute-start(bf16[512,1024]{1,0:T(8,128)(2,1)S(1)} %collective-permute-done.1.t2), channel_id=1, source_target_pairs={{0,1},{1,0},{2,3},{3,2},{4,5},{5,4},{6,7},{7,6},{8,9},{9,8},{10,11... | collective-permute-start | bytes 3145736 | tf_op jit(solution)/shard_map/ppermute | solution.py:131
  61.6 8.2 %all-to-all-start.1 = ((s16[8,32,128]{2,1,0:T(8,128)(2,1)}), s16[8,32,128]{2,1,0:T(8,128)(2,1)S(1)}, u32[]{:S(2)}, u32[]{:S(2)}) async-start(s16[8,32,128]{2,1,0:T(8,128)(2,1)} %broadcast_in_dim.14), calls=%async_computation.1 | async-start | bytes 131072 | tf_op jit(solution)/shard_map/all_to_all | solution.py:147
  69.8 7.1 %all-to-all-done.1 = s16[8,32,128]{2,1,0:T(8,128)(2,1)S(1)} async-done(((s16[8,32,128]{2,1,0:T(8,128)(2,1)}), s16[8,32,128]{2,1,0:T(8,128)(2,1)S(1)}, u32[]{:S(2)}, u32[]{:S(2)}) %all-to-all-start.1) | async-done | bytes 65568 | tf_op jit(solution)/shard_map/all_to_all | solution.py:147
  77.6 8.3 %count.2.w_ref = bf16[8,4096,128]{2,1,0:T(8,128)(2,1)} custom-call(s32[32,8,128]{2,1,0:T(8,128)} %fusion.14.keys_ref), custom_call_target="tpu_custom_call" | custom-call | tf_op jit(solution)/shard_map/count/pallas_call | solution.py:65
  85.9 1.0 copy-done.3
  86.9 9.3 %pool.1 = f32[8,512,128]{2,1,0:T(8,128)} custom-call(bf16[512,1024]{1,0:T(8,128)(2,1)} %bitcast.30, bf16[512,1024]{1,0:T(8,128)(2,1)} %copy-done.3, bf16[512,1024]{1,0:T(8,128)(2,1)} %copy-done.2, bf16[512,1024]{1,0:T(8,128)(2,1)} %collective-permute-done.2.t3, bf16[8,4096,128]{2,1,0:T(8,128)(2,1)} %count.2.w_ref), custom_call_target="tpu_custom_call" | custom-call | tf_op jit(solution)/shard_map/pool/pallas_call | solution.py:92
  96.2 2.3 %copy.11 = bf16[1024,512]{1,0:T(8,128)(2,1)} copy(bf16[1024,512]{0,1:T(8,128)(2,1)} %bitcast.31) | data formatting | bytes 2097152 | tf_op jit(solution)/shard_map/transpose | solution.py:160
  98.5 7.2 %all-to-all-start.2 = ((bf16[32,32,512]{2,1,0:T(8,128)(2,1)}), bf16[32,32,512]{2,1,0:T(8,128)(2,1)S(1)}, u32[]{:S(2)}, u32[]{:S(2)}) async-start(bf16[32,32,512]{2,1,0:T(8,128)(2,1)} %bitcast.17), calls=%async_computation.3 | async-start | bytes 2097152 | tf_op jit(solution)/shard_map/all_to_all | solution.py:160
  105.9 4.1 %collective-permute-done.3 = s16[8,32,128]{2,1,0:T(8,128)(2,1)S(1)} collective-permute-done((s16[8,32,128]{2,1,0:T(8,128)(2,1)S(1)}, s16[8,32,128]{2,1,0:T(8,128)(2,1)S(1)}, u32[]{:S(2)}, u32[]{:S(2)}) %collective-permute-start.3) | collective-permute-done | bytes 65568 | tf_op jit(solution)/shard_map/ppermute | solution.py:131
  112.7 1.2 copy.10
  113.9 10.5 %count.3.w_ref = bf16[32,1024,128]{2,1,0:T(8,128)(2,1)} custom-call(s32[32,32,128]{2,1,0:T(8,128)} %bitcast.33), custom_call_target="tpu_custom_call" | custom-call | tf_op jit(solution)/shard_map/count/pallas_call | solution.py:65
  124.4 21.6 %all-to-all-done.2.pieces_ref = bf16[32,32,512]{2,1,0:T(8,128)(2,1)S(1)} async-done(((bf16[32,32,512]{2,1,0:T(8,128)(2,1)}), bf16[32,32,512]{2,1,0:T(8,128)(2,1)S(1)}, u32[]{:S(2)}, u32[]{:S(2)}) %all-to-all-start.2) | async-done | bytes 1048608 | tf_op jit(solution)/shard_map/all_to_all | solution.py:160
  146.0 1.0 copy-done.1
  147.0 10.1 %update.1 = bf16[32,32,512]{2,1,0:T(8,128)(2,1)} custom-call(s32[1]{0:T(128)} %dynamic_slice.3.shift_ref, bf16[32,1024,128]{2,1,0:T(8,128)(2,1)} %count.3.w_ref, bf16[4096,512]{1,0:T(8,128)(2,1)} %all-gather.2.cloned.1.call-done.grads_ref, bf16[32,32,512]{2,1,0:T(8,128)(2,1)} %copy-done.1), custom_call_target="tpu_custom_call" | custom-call | tf_op jit(solution)/shard_map/update/pallas_call | solution.py:113
  157.0 4.3 %all-to-all-start.3 = ((bf16[32,32,512]{2,1,0:T(8,128)(2,1)}), bf16[32,32,512]{2,1,0:T(8,128)(2,1)S(1)}, u32[]{:S(2)}, u32[]{:S(2)}) async-start(bf16[32,32,512]{2,1,0:T(8,128)(2,1)} %update.1), calls=%async_computation.4 | async-start | bytes 2097152 | tf_op jit(solution)/shard_map/all_to_all | solution.py:169
  161.4 1.0 convert_bitcast_fusion
  163.1 27.2 %all-to-all-done.3 = bf16[32,32,512]{2,1,0:T(8,128)(2,1)S(1)} async-done(((bf16[32,32,512]{2,1,0:T(8,128)(2,1)}), bf16[32,32,512]{2,1,0:T(8,128)(2,1)S(1)}, u32[]{:S(2)}, u32[]{:S(2)}) %all-to-all-start.3) | async-done | bytes 1048608 | tf_op jit(solution)/shard_map/all_to_all | solution.py:169
  190.3 1.0 copy.15
  (27 shorter events, 6.0 us)
Async XLA Ops:
  8.0 138.0 %all-gather.2.cloned.1.call-start = ((), (), s32[]{:S(2)}) async-start(), calls=%async_computation.6 | async-start | bytes 4456448 | tf_op jit(solution)/shard_map/all_gather | solution.py:142
  8.0 4.5 %collective-permute-start.5 = (bf16[128,512]{1,0:T(8,128)(2,1)}, bf16[128,512]{1,0:T(8,128)(2,1)S(1)}, u32[]{:S(2)}, u32[]{:S(2)}) collective-permute-start(bf16[128,512]{1,0:T(8,128)(2,1)} %bitcast.36), channel_id=1, source_target_pairs={{0,2},{2,0},{1,3},{3,1},{4,6},{6,4},{5,7},{7,5},{8,10},{10,8},{9,1... | collective-permute-start | bytes 393224 | tf_op jit(solution)/shard_map/ppermute | solution.py:131
  34.6 51.3 %copy-start = (bf16[8,64,1024]{2,1,0:T(8,128)(2,1)}, bf16[8,64,1024]{2,1,0:T(8,128)(2,1)S(1)}, u32[]{:S(2)}) copy-start(bf16[8,64,1024]{2,1,0:T(8,128)(2,1)S(1)} %all_to_all.20) | copy-start | bytes 3145732
  34.6 21.2 %collective-permute-start.1 = (bf16[512,1024]{1,0:T(8,128)(2,1)S(1)}, bf16[512,1024]{1,0:T(8,128)(2,1)S(1)}, u32[]{:S(2)}, u32[]{:S(2)}) collective-permute-start(bf16[512,1024]{1,0:T(8,128)(2,1)S(1)} %bitcast.28), channel_id=1, source_target_pairs={{0,2},{2,0},{1,3},{3,1},{4,6},{6,4},{5,7},{7,5},{8,10},{10,8},{9,1... | collective-permute-start | bytes 3145736 | tf_op jit(solution)/shard_map/ppermute | solution.py:131
  35.8 50.1 %collective-permute-start = (bf16[512,1024]{1,0:T(8,128)(2,1)S(1)}, bf16[512,1024]{1,0:T(8,128)(2,1)S(1)}, u32[]{:S(2)}, u32[]{:S(2)}) collective-permute-start(bf16[512,1024]{1,0:T(8,128)(2,1)S(1)} %bitcast.29), channel_id=1, source_target_pairs={{0,1},{1,0},{2,3},{3,2},{4,5},{5,4},{6,7},{7,6},{8,9},{9,8},{10,11... | collective-permute-start | bytes 3145736 | tf_op jit(solution)/shard_map/ppermute | solution.py:131
  55.8 30.1 %copy-start.2 = (bf16[512,1024]{1,0:T(8,128)(2,1)}, bf16[512,1024]{1,0:T(8,128)(2,1)S(1)}, u32[]{:S(2)}) copy-start(bf16[512,1024]{1,0:T(8,128)(2,1)S(1)} %collective-permute-done.1.t2) | copy-start | bytes 3145732
  55.8 30.0 %collective-permute-start.2 = (bf16[512,1024]{1,0:T(8,128)(2,1)S(1)}, bf16[512,1024]{1,0:T(8,128)(2,1)}, u32[]{:S(2)}, u32[]{:S(2)}) collective-permute-start(bf16[512,1024]{1,0:T(8,128)(2,1)S(1)} %collective-permute-done.1.t2), channel_id=1, source_target_pairs={{0,1},{1,0},{2,3},{3,2},{4,5},{5,4},{6,7},{7,6},{8,9},{9,8},{10,11... | collective-permute-start | bytes 3145736 | tf_op jit(solution)/shard_map/ppermute | solution.py:131
  61.6 15.3 %all-to-all-start.1 = ((s16[8,32,128]{2,1,0:T(8,128)(2,1)}), s16[8,32,128]{2,1,0:T(8,128)(2,1)S(1)}, u32[]{:S(2)}, u32[]{:S(2)}) async-start(s16[8,32,128]{2,1,0:T(8,128)(2,1)} %broadcast_in_dim.14), calls=%async_computation.1 | async-start | bytes 131072 | tf_op jit(solution)/shard_map/all_to_all | solution.py:147
  69.8 91.6 %reduce-scatter.2.cloned.1.call-start = ((), (), s32[]{:S(2)}) async-start(), calls=%async_computation.5 | async-start | bytes 2359296 | tf_op jit(solution)/shard_map/reduce_scatter | solution.py:157
  85.9 24.9 %copy-start.4 = (s32[8]{0:T(128)S(1)}, s32[8]{0:T(128)}, u32[]{:S(2)}) copy-start(s32[8]{0:T(128)} %param.6) | copy-start | bytes 100
  85.9 1.0 copy-start.3
  98.5 47.5 %all-to-all-start.2 = ((bf16[32,32,512]{2,1,0:T(8,128)(2,1)}), bf16[32,32,512]{2,1,0:T(8,128)(2,1)S(1)}, u32[]{:S(2)}, u32[]{:S(2)}) async-start(bf16[32,32,512]{2,1,0:T(8,128)(2,1)} %bitcast.17), calls=%async_computation.3 | async-start | bytes 2097152 | tf_op jit(solution)/shard_map/all_to_all | solution.py:160
  105.7 4.3 %collective-permute-start.3 = (s16[8,32,128]{2,1,0:T(8,128)(2,1)S(1)}, s16[8,32,128]{2,1,0:T(8,128)(2,1)S(1)}, u32[]{:S(2)}, u32[]{:S(2)}) collective-permute-start(s16[8,32,128]{2,1,0:T(8,128)(2,1)S(1)} %all-to-all-done.1), channel_id=1, source_target_pairs={{0,2},{2,0},{1,3},{3,1},{4,6},{6,4},{5,7},{7,5},{8,10},{10,8},{9,1... | collective-permute-start | bytes 196616 | tf_op jit(solution)/shard_map/ppermute | solution.py:131
  110.0 1.8 collective-permute-start.4
  146.0 1.0 copy-start.1
  157.0 33.2 %all-to-all-start.3 = ((bf16[32,32,512]{2,1,0:T(8,128)(2,1)}), bf16[32,32,512]{2,1,0:T(8,128)(2,1)S(1)}, u32[]{:S(2)}, u32[]{:S(2)}) async-start(bf16[32,32,512]{2,1,0:T(8,128)(2,1)} %update.1), calls=%async_computation.4 | async-start | bytes 2097152 | tf_op jit(solution)/shard_map/all_to_all | solution.py:169
Sparse Core Ops, SparseCore 0:
  14.3 46.4 all-gather.1
Sparse Core Ops, SparseCore 1:
  96.3 53.8 reduce-scatter.1
